TPU v7x, 32 devices: a whole 2x2x4 slice. The times are simulated.
32 devices in a mesh: aux: 8 (over y, x, core), pair: 4 (over z).
Axes of the slice: x: 2, y: 2, z: 4, core: 2. Of those that a mesh axis runs over, the one named last changes fastest.
Arguments:
- integrals: bfloat16 [3072, 32768], P('aux', 'pair'), may hold values from -0.15625 to 0.15625
- densities: bfloat16 [16, 32768], P(None, 'pair'), may hold values from -2.390625 to 2.390625
- screen: int32 [24, 256], P('aux', 'pair'), may hold values 0 or 1
- factor: float32 [3072, 3072], P('aux', 'pair'), may hold values from -0.109375 to 0.109375
- diag_inv: float32 [3072, 768], P('aux'), may hold values from -2 to 2, as said below
Outputs:
- coulomb: float32 [16, 32768], P(None, ('pair', 'aux'))
Inputs may be any that keep to these rules, and one draw needn't show every extreme that they name: `diag_inv`: each block of 768 rows is an upper triangular matrix with a positive diagonal.
All inputs are finite; a program needn't handle non-finite values. No bound on the sum of `screen` on one device may be relied on, other than what follows from the above.
Results may differ from a plain program's by a relative error of at most 0.0041.
Values may be sent and summed in bfloat16 or wider, within the bound.
No kernel may reach another device: no remote copies, remote signals or barrier semaphores. Data moves between devices by JAX's collectives and lax.ppermute only.
A program may use at most 128 MiB of HBM per device.

v0:
```python
import functools

import jax
import jax.numpy as jnp
from jax import lax
from jax.experimental import pallas as pl
from jax.experimental.pallas import tpu as pltpu
from jax.sharding import PartitionSpec as P

TILE = 128
SOLVE_BLOCKS = 4
AXES = ("aux", "pair")
HIGHEST = lax.Precision.HIGHEST
F32 = jnp.float32
BF16 = jnp.bfloat16
VMEM = pl.BlockSpec(memory_space=pltpu.VMEM)
SMEM = pl.BlockSpec(memory_space=pltpu.SMEM)
HBM = pl.BlockSpec(memory_space=pltpu.HBM)
MIB = 1024 * 1024
NN = (((1,), (0,)), ((), ()))
NT = (((1,), (1,)), ((), ()))
TN = (((0,), (0,)), ((), ()))


def struct(shape, dtype=F32):
    return jax.ShapeDtypeStruct(shape, dtype)


def call(kernel, outs, *operands, limit=12, specs=None, scratch=()):
    return pl.pallas_call(
        kernel,
        out_shape=outs,
        in_specs=specs or [VMEM] * len(operands),
        out_specs=jax.tree.map(lambda _: VMEM, outs),
        scratch_shapes=scratch,
        compiler_params=pltpu.CompilerParams(vmem_limit_bytes=limit * MIB),
    )(*operands)


def side_of():
    return lax.rem(lax.axis_index("aux"), 2)


def block_of():
    return lax.div(lax.axis_index("aux"), 2)


def masked_row(screen, densities, i, tiles):
    zero = jnp.zeros((), densities.dtype)
    return jnp.concatenate(
        [
            jnp.where(screen[i, t] != 0, densities[:, t * TILE : (t + 1) * TILE], zero)
            for t in tiles
        ],
        axis=1,
    )


def fit(
    screen_in, densities_in, integrals, left, right, out, screen, densities, total, arrived
):
    height, width = integrals.shape
    pieces = arrived.shape[0] - 2
    chunk = width // pieces
    small = [
        pltpu.make_async_copy(screen_in, screen, arrived.at[pieces]),
        pltpu.make_async_copy(densities_in, densities, arrived.at[pieces + 1]),
    ]
    copies = []
    held = []
    for j in range(pieces):
        ref = left if 2 * j < pieces else right
        start = j * chunk if ref is left else j * chunk - width // 2
        held.append(ref.at[:, start : start + chunk])
        copies.append(
            pltpu.make_async_copy(
                integrals.at[:, j * chunk : (j + 1) * chunk], held[j], arrived.at[j]
            )
        )
    for copy in small + copies:
        copy.start()
    total[...] = jnp.zeros_like(total)
    for copy in small:
        copy.wait()
    count = densities.shape[0]
    strips = height // TILE
    for j in range(pieces):
        tiles = range(j * chunk // TILE, (j + 1) * chunk // TILE)
        stacked = jnp.concatenate([masked_row(screen, densities, i, tiles) for i in range(strips)])
        copies[j].wait()
        total[...] += lax.dot_general(held[j][...], stacked, NT, preferred_element_type=F32)
    done = total[...].T
    for i in range(strips):
        out[:, i * TILE : (i + 1) * TILE] = done[
            i * count : (i + 1) * count, i * TILE : (i + 1) * TILE
        ]


def fit_partial(densities, integrals, screen):
    count = densities.shape[0]
    height, width = integrals.shape
    pieces = 4 if width % (4 * TILE) == 0 else width // TILE
    return call(
        fit,
        [struct((height, width // 2), BF16)] * 2 + [struct((count, height))],
        *(pltpu.with_memory_space_constraint(x, pltpu.HBM) for x in (screen, densities, integrals)),
        specs=[HBM] * 3,
        scratch=[
            pltpu.SMEM(screen.shape, jnp.int32),
            pltpu.VMEM(densities.shape, BF16),
            pltpu.VMEM((height, height // TILE * count), F32),
            pltpu.SemaphoreType.DMA((pieces + 2,)),
        ],
    )


def slab(screen, stacked, left, right, member, members):
    strips = left.shape[0] // TILE
    count = stacked.shape[0] // strips
    chunk = 2 * left.shape[1] // members
    held, first = (left, member) if 2 * member < members else (right, member - members // 2)
    columns = slice(first * chunk, (first + 1) * chunk)
    parts = jnp.dot(stacked, held[:, columns], preferred_element_type=F32)
    tiles = []
    for t in range(chunk // TILE):
        total = jnp.zeros((count, TILE), F32)
        for i in range(strips):
            part = parts[i * count : (i + 1) * count, t * TILE : (t + 1) * TILE]
            total += jnp.where(screen[i, member * (chunk // TILE) + t] != 0, part, 0.0)
        tiles.append(total)
    return jnp.concatenate(tiles, axis=1)


def by_strip(value, strips):
    strip_of = lax.broadcasted_iota(jnp.int32, value.shape, 1) // TILE
    return jnp.concatenate(
        [jnp.where(strip_of == i, value, jnp.zeros((), BF16)) for i in range(strips)]
    )


def coulomb(screen, rounded, left, right, out):
    members = out.shape[0]
    stacked = by_strip(rounded[...], left.shape[0] // TILE)
    for m in range(members):
        out[m] = slab(screen, stacked, left, right, m, members).astype(out.dtype)


def coulomb_side(wanted, screen, rounded, left, right, out):
    chips = out.shape[0]
    stacked = by_strip(rounded[...], left.shape[0] // TILE)

    def compute(side):
        for k in range(chips):
            part = slab(screen, stacked, left, right, 2 * k + side, 2 * chips)
            out[k] = part.astype(out.dtype)

    for side in range(2):
        pl.when(wanted == side)(functools.partial(compute, side))


def coulomb_mate(*refs):
    coulomb_side(1 - side_of(), *refs)


def coulomb_own(*refs):
    coulomb_side(side_of(), *refs)


def share(own, got, keep, one, two, three):
    block = block_of()
    keep[...] = own[block] + got[block].astype(F32)
    for distance, out in ((1, one), (2, two), (3, three)):
        chip = lax.bitwise_xor(block, distance)
        out[...] = (own[chip] + got[chip].astype(F32)).astype(out.dtype)


def gather_up(keep, one, two, three, out):
    out[...] = keep[...] + one[...].astype(F32) + two[...].astype(F32) + three[...].astype(F32)


def coulomb_partial(rounded, left, right, screen):
    members = lax.axis_size("aux")
    out = struct((members, rounded.shape[0], 2 * left.shape[1] // members), BF16)
    return call(coulomb, out, screen, rounded, left, right, specs=[SMEM, VMEM, VMEM, VMEM])


def chip_coulomb(rounded, left, right, screen):
    members = 2 * SOLVE_BLOCKS
    count = rounded.shape[0]
    chunk = 2 * left.shape[1] // members
    specs = [SMEM, VMEM, VMEM, VMEM]
    operands = (screen, rounded, left, right)
    given = call(coulomb_mate, struct((SOLVE_BLOCKS, count, chunk), BF16), *operands, specs=specs)

    def move(value, to):
        return lax.ppermute(value, "aux", [(i, to(i)) for i in range(members)])

    got = move(given, lambda i: i ^ 1)
    own = call(coulomb_own, struct((SOLVE_BLOCKS, count, chunk)), *operands, specs=specs)
    piece = struct((count, chunk), BF16)
    keep, one, two, three = call(share, [struct((count, chunk))] + [piece] * 3, own, got)
    three = move(three, lambda i: i ^ 6)
    one = move(one, lambda i: i ^ 2)
    two = move(two, lambda i: i ^ 4)
    return call(gather_up, struct((count, chunk)), keep, one, two, three)


def scatter_sum(slabs):
    arrived = lax.all_to_all(slabs, "aux", 0, 0, tiled=True)
    return jnp.sum(arrived.astype(F32), axis=0)


def high_low(value):
    high = value.astype(BF16)
    return high, (value - high.astype(F32)).astype(BF16)


def times(value, high, low, dims=NN):
    rows = value.shape[0]
    coarse = value.astype(BF16).astype(F32)
    pair = jnp.concatenate([coarse, value - coarse], axis=0).astype(BF16)
    both = lax.dot_general(pair, high, dims, preferred_element_type=F32)
    both += lax.dot_general(pair, low, dims, preferred_element_type=F32)
    return both[:rows] + both[rows:]


def prepare_first(*refs):
    here = (block_of() == 0) | (lax.axis_index("pair") > 0)
    prepare(here, *refs)


def prepare_later(*refs):
    prepare(lax.axis_index("pair") == 0, *refs)


def prepare(here, inv0, inv1, fac0, fac1, k_high, k_low, kt_high, kt_low, lhs, rhs):
    height = inv0.shape[0]

    @pl.when(here & (block_of() > 0) & (side_of() == 0))
    def _():
        for n, (inv, fac) in enumerate(((inv0, fac0), (inv1, fac1))):
            rows = [slice((3 * n + r) * height, (3 * n + r + 1) * height) for r in range(3)]
            high, low = high_low(inv[...])
            lhs[rows[0], :], lhs[rows[1], :], lhs[rows[2], :] = high, low, high
            high, low = high_low(fac[...])
            rhs[rows[0], :], rhs[rows[1], :], rhs[rows[2], :] = high, high, low
        depth = 3 * height
        halves = (
            (slice(0, height), slice(0, depth)),
            (slice(height, 2 * height), slice(0, 2 * depth)),
        )
        for part, used in halves:
            product = lax.dot_general(lhs[used, part], rhs[used, :], TN, preferred_element_type=F32)
            k_high[part, :], k_low[part, :] = high_low(product)
            kt_high[:, part], kt_low[:, part] = high_low(product.T)


def begin(f0, f1, f2, f3, inv, after, out):
    high, low = high_low(inv[...])
    out[...] = times(f0[...] + f1[...] + f2[...] + f3[...], high, low)


def both(own, mate, out):
    out[...] = own[...] + mate[...]


def lead_only(kernel):
    @functools.wraps(kernel)
    def guarded(*refs):
        pl.when(side_of() == 0)(lambda: kernel(*refs))

    return guarded


@lead_only
def after_zero(one, two, three, e, high, low, out):
    block = block_of()
    known = jnp.where(block == 1, one[...], jnp.where(block == 2, two[...], three[...]))
    term = times(known, high[...], low[...])
    out[...] = jnp.where(block == 0, e[...], jnp.where(block == 1, two[...] - term, term))


@lead_only
def after_one(first, second, e, high, low, out):
    block = block_of()
    known = jnp.where(block == 3, second[...], first[...])
    behind = jnp.where(block == 3, first[...], second[...])
    total = behind + times(known, high[...], low[...])
    out[...] = jnp.where(block == 0, e[...], jnp.where(block == 3, total, e[...] - total))


@lead_only
def turn(known, behind, e, kt_high, kt_low, high, low, settled, back):
    value = e[...] - behind[...] - times(known[...], kt_high[...], kt_low[...])
    settled[...] = value
    back[...] = times(value, high[...], low[...])


@lead_only
def back_two(into, near, far, t, s, high, low, high0, low0, settled, back, mixed):
    plane = lax.axis_index("pair")
    last = block_of() == 3
    passed = jnp.where(plane == 0, far[...], jnp.where(plane == 1, near[...], t[...]))
    value = jnp.where(last, passed, s[...] - into[...])
    settled[...] = value

    def multiply(high, low):
        product = times(value, high[...], low[...])
        back[...] = product
        mixed[...] = jnp.where(last, product, value)

    pl.when(plane == 0)(lambda: multiply(high0, low0))
    pl.when(plane > 0)(lambda: multiply(high, low))


@lead_only
def back_one(into, other, t, s, high, low, settled, back):
    plane = lax.axis_index("pair")
    block = block_of()
    passed = jnp.where(plane == 0, other[...], t[...])
    value = jnp.where(
        block == 1,
        s[...] - into[...] - other[...],
        jnp.where(block == 2, passed, t[...]),
    )
    settled[...] = value
    product = times(value, high[...], low[...])
    back[...] = jnp.where(block == 2, product + into[...], product)


def collect(z0, z1, z2, z3, i0, i1, i2, i3, t, p1, p2, p3, out):
    plane = lax.axis_index("pair")
    block = block_of()

    def by_plane(a, b, c, d):
        return jnp.where(
            plane == 0, a[...], jnp.where(plane == 1, b[...], jnp.where(plane == 2, c[...], d[...]))
        )

    start = by_plane(z0, z1, z2, z3)
    zero = start - by_plane(i0, i1, i2, i3) - by_plane(i3, i0, i1, i2)
    one = by_plane(t, p1, p2, p3)
    two = by_plane(t, t, p1, p2)
    three = by_plane(t, t, t, p1)
    out[...] = jnp.where(
        block == 0, zero, jnp.where(block == 1, one, jnp.where(block == 2, two, three))
    )


def finish(own, mate, inv, out):
    value = jnp.where(side_of() == 0, own[...], mate[...])
    high, low = high_low(inv[...])
    out[...] = times(value, high, low, NT).astype(out.dtype)


def mm(a, b):
    return jnp.dot(a, b, precision=HIGHEST, preferred_element_type=F32)


def mm_t(a, b):
    return lax.dot_general(a, b, NT, precision=HIGHEST, preferred_element_type=F32)


def chip_solve(partial_fit, factor, diag_inv):
    count, height = partial_fit.shape
    size = 2 * height
    planes = lax.axis_size("pair")
    chips = [(k, plane) for k in range(SOLVE_BLOCKS) for plane in range(planes)]

    def device(chip, c):
        return (2 * chip[0] + c) * planes + chip[1]

    def permute(value, to):
        for chip in chips:
            for c in range(2):
                to.setdefault(device(chip, c), device(chip, 1 - c))
        return lax.ppermute(value, AXES, sorted(to.items()))

    def send(value, *moves):
        to = {}
        for source, target, *via in moves:
            loop = [device(source, 0), device(target, 0), device(target, 1)]
            for chip in via:
                loop += [device(chip, 0), device(chip, 1)]
            loop.append(device(source, 1))
            to.update(zip(loop, loop[1:] + loop[:1]))
        return permute(value, to)

    def swap(value):
        return lax.ppermute(value, "aux", [(i, i ^ 1) for i in range(2 * SOLVE_BLOCKS)])

    panel = struct((count, size))
    square = struct((size, size), BF16)
    home = [1, 1, 1, 2]
    gathered = []
    for route in ("far", "other", "middle"):
        to = {}
        for k in range(SOLVE_BLOCKS):
            turn_to = 1 if home[k] < 2 else -1
            middle, far, other = home[k] + turn_to, home[k] + 2 * turn_to, home[k] - turn_to
            ring = {"far": (far, home[k], middle), "middle": (middle, home[k]), "other": (other, home[k])}
            for c in range(2):
                loop = [device((k, plane), c) for plane in ring[route]]
                to.update(zip(loop, loop[1:] + loop[:1]))
        gathered.append(permute(partial_fit, to))
    halves = (diag_inv, permute(diag_inv, {}), factor, permute(factor, {}))

    def prepared(kernel):
        scratch = [pltpu.VMEM((3 * size, size), BF16)] * 2
        return call(kernel, [square] * 4, *halves, limit=32, scratch=scratch)

    k_high, k_low, kt_high, kt_low = prepared(prepare_first)
    at_zero = prepared(prepare_later)
    e = call(begin, panel, partial_fit, *gathered, diag_inv, k_high)
    e = call(both, panel, e, swap(e))
    reach = [
        send(e, ((0, 1), (1, 0))),
        send(e, ((0, 1), (2, 0)), ((1, 1), (1, 0))),
        send(e, ((0, 1), (3, 0))),
    ]
    one = call(after_zero, panel, *reach, e, *at_zero[2:])
    first = send(one, ((1, 0), (2, 1)), ((3, 0), (3, 1)), ((0, 1), (0, 0)))
    second = send(one, ((1, 0), (3, 1)), ((2, 0), (2, 1)), ((0, 1), (0, 2)))
    two = call(after_one, panel, first, second, e, kt_high, kt_low)
    behind = send(two, ((3, 1), (3, 2)), ((0, 1), (0, 3)))
    known = send(two, ((2, 1), (3, 2), (2, 2)))
    t, back = call(turn, [panel] * 2, known, behind, e, kt_high, kt_low, k_high, k_low)
    into = send(back, ((3, 2), (2, 1)))
    near = send(t, ((3, 2), (3, 1)))
    far = send(t, ((3, 2), (3, 0)))
    t, back, mixed = call(back_two, [panel] * 3, into, near, far, t, two, k_high, k_low, *at_zero[:2])
    into = send(back, ((2, 1), (1, 0)), ((3, 0), (2, 0)))
    other = send(mixed, ((3, 1), (1, 0)), ((2, 1), (2, 0)))
    t, back = call(back_one, [panel] * 2, into, other, t, one, *at_zero[:2])
    near = {
        ((1, 0), (0, 3)): (3, 0),
        ((1, 0), (0, 2)): (1, 1),
        ((2, 0), (0, 3)): (2, 1),
        ((2, 0), (0, 2)): (3, 1),
        ((2, 0), (0, 0)): (2, 2),
    }
    into = [None] * planes
    spread = [None] * planes

    def spread_to(step):
        moves = [((1, 0), (1, step))]
        if 1 + step < planes:
            moves.append(((2, 1), (2, 1 + step)))
        if 2 + step < planes:
            moves.append(((3, 2), (3, 2 + step)))
        spread[step] = send(t, *moves)

    spread_to(planes - 1)
    for plane in reversed(range(planes)):
        moves = [((1, 0), (0, plane)), ((2, 0), (0, (plane + 1) % planes))]
        into[plane] = send(
            back, *((*move, near[move]) if move in near else move for move in moves)
        )
    for step in reversed(range(1, planes - 1)):
        spread_to(step)
    t = call(collect, panel, first, e, second, behind, *into, t, *spread[1:])
    return call(finish, struct((count, height), BF16), t, swap(t), diag_inv)


def chain_solve(partial_fit, factor, diag_inv):
    count, height = partial_fit.shape
    breadth = factor.shape[1]
    block_size = diag_inv.shape[1]
    rows_aux = lax.axis_size("aux")
    total = height * rows_aux
    members = rows_aux // SOLVE_BLOCKS
    my_row = lax.axis_index("aux")
    my_column = lax.axis_index("pair")
    my_block = my_row // members
    column_block = (my_column * breadth + jnp.arange(breadth, dtype=jnp.int32)) // block_size
    factor_low = jnp.where((column_block < my_block)[None, :], factor, 0.0)

    def own_columns(whole):
        return lax.dynamic_slice_in_dim(whole, my_column * breadth, breadth, 1)

    zero_block = jnp.zeros((count, block_size), jnp.float32)
    solved = jnp.zeros((count, total), jnp.float32)
    for k in range(SOLVE_BLOCKS):

        def on_group(current):
            return mm(partial_fit - mm_t(own_columns(current), factor_low), diag_inv)

        def off_group(current):
            return zero_block

        summand = lax.cond(my_block == k, on_group, off_group, solved)
        arrived = lax.psum(summand, AXES)
        solved = lax.dynamic_update_slice_in_dim(solved, arrived, k * block_size, 1)
    own_coef = jnp.zeros((count, height), jnp.float32)
    contrib = jnp.zeros((count, total), jnp.float32)
    for target in reversed(range(SOLVE_BLOCKS)):
        settled = solved[:, target * block_size : (target + 1) * block_size]
        if target < SOLVE_BLOCKS - 1:
            portion = contrib[:, target * block_size : (target + 1) * block_size]
            settled = settled - lax.psum(portion, AXES)

        def on_group(state):
            coef = mm_t(settled, diag_inv)
            if target > 0:
                fresh = lax.dynamic_update_slice_in_dim(
                    jnp.zeros((count, total), jnp.float32),
                    mm(coef, factor_low),
                    my_column * breadth,
                    1,
                )
            else:
                fresh = state[1]
            return (coef, fresh)

        def keep_state(state):
            return state

        own_coef, contrib = lax.cond(my_block == target, on_group, keep_state, (own_coef, contrib))
    return own_coef.astype(jnp.bfloat16)


def shards(integrals, densities, screen, factor, diag_inv):
    block_size = diag_inv.shape[1]
    chip_blocks = (
        lax.axis_size("aux") == 2 * SOLVE_BLOCKS
        and factor.shape[1] == block_size
        and lax.axis_size("pair") == SOLVE_BLOCKS
    )
    solve = chip_solve if chip_blocks else chain_solve
    left, right, partial_fit = fit_partial(densities, integrals, screen)
    rounded = solve(partial_fit, factor, diag_inv)
    if chip_blocks:
        return chip_coulomb(rounded, left, right, screen)
    return scatter_sum(coulomb_partial(rounded, left, right, screen))


def solution(mesh):
    in_specs = (
        P("aux", "pair"),
        P(None, "pair"),
        P("aux", "pair"),
        P("aux", "pair"),
        P("aux", None),
    )
    out_specs = P(None, ("pair", "aux"))
    return jax.shard_map(shards, mesh=mesh, in_specs=in_specs, out_specs=out_specs, check_vma=False)
```

profile of v0, /device:TPU:0, one launch (start us, length us, event | category | flops | bytes accessed | tf_op | source)
XLA Modules:
  0.0 58.8 jit_solution(16447931095880532443)
XLA Ops:
  0.0 0.5 collective-permute-start.4
  0.6 4.0 %shard_map.55 = (bf16[384,4096]{1,0:T(8,128)(2,1)S(1)}, bf16[384,4096]{1,0:T(8,128)(2,1)S(1)}, f32[16,384]{1,0:T(8,128)S(1)}) custom-call(s32[3,64]{1,0:T(4,128)} %refs_0_.7, bf16[16,8192]{1,0:T(8,128)(2,1)} %densities_in.1, bf16[384,8192]{1,0:T(8,128)(2,1)} %integrals.1), custom_call_target="tpu_custom_call" | custom-call | tf_op jit(solution)/shard_map/pallas_call | solution.py:30
  4.6 0.6 collective-permute-start.2
  5.1 4.1 %collective-permute-start.1 = (f32[16,384]{1,0:T(8,128)S(1)}, f32[16,384]{1,0:T(8,128)S(1)}, u32[]{:S(2)}, u32[]{:S(2)}) collective-permute-start(f32[16,384]{1,0:T(8,128)S(1)} %get-tuple-element.27.f0), channel_id=1, source_target_pairs={{0,1},{1,0},{2,6},{3,7},{4,5},{5,4},{6,2},{7,3},{8,9},{9,8},{10,14... | collective-permute-start | bytes 73736 | tf_op jit(solution)/shard_map/ppermute | solution.py:377
  9.4 1.7 %collective-permute-done.1.f2 = f32[16,384]{1,0:T(8,128)S(1)} collective-permute-done((f32[16,384]{1,0:T(8,128)S(1)}, f32[16,384]{1,0:T(8,128)S(1)}, u32[]{:S(2)}, u32[]{:S(2)}) %collective-permute-start.1) | collective-permute-done | bytes 24608 | tf_op jit(solution)/shard_map/ppermute | solution.py:377
  11.4 1.2 %collective-permute-done.5.mate = f32[16,768]{1,0:T(8,128)S(1)} collective-permute-done((f32[16,768]{1,0:T(8,128)S(1)}, f32[16,768]{1,0:T(8,128)S(1)}, u32[]{:S(2)}, u32[]{:S(2)}) %collective-permute-start.5) | collective-permute-done | bytes 49184 | tf_op jit(solution)/shard_map/ppermute | solution.py:390
  13.3 0.6 %collective-permute-done.8.three = f32[16,768]{1,0:T(8,128)S(1)} collective-permute-done((f32[16,768]{1,0:T(8,128)S(1)}, f32[16,768]{1,0:T(8,128)S(1)}, u32[]{:S(2)}, u32[]{:S(2)}) %collective-permute-start.8) | collective-permute-done | bytes 49184 | tf_op jit(solution)/shard_map/ppermute | solution.py:377
  15.0 0.5 collective-permute-start.9
  15.5 0.7 %collective-permute-done.10.second.z2 = f32[16,768]{1,0:T(8,128)S(1)} collective-permute-done((f32[16,768]{1,0:T(8,128)S(1)}, f32[16,768]{1,0:T(8,128)S(1)}, u32[]{:S(2)}, u32[]{:S(2)}) %collective-permute-start.10) | collective-permute-done | bytes 49184 | tf_op jit(solution)/shard_map/ppermute | solution.py:377
  16.2 6.6 %collective-permute-done.9.first.z0 = f32[16,768]{1,0:T(8,128)S(1)} collective-permute-done((f32[16,768]{1,0:T(8,128)S(1)}, f32[16,768]{1,0:T(8,128)S(1)}, u32[]{:S(2)}, u32[]{:S(2)}) %collective-permute-start.9) | collective-permute-done | bytes 49184 | tf_op jit(solution)/shard_map/ppermute | solution.py:377
  23.3 0.5 collective-permute-start.11
  23.8 0.7 %collective-permute-done.12.known = f32[16,768]{1,0:T(8,128)S(1)} collective-permute-done((f32[16,768]{1,0:T(8,128)S(1)}, f32[16,768]{1,0:T(8,128)S(1)}, u32[]{:S(2)}, u32[]{:S(2)}) %collective-permute-start.12) | collective-permute-done | bytes 49184 | tf_op jit(solution)/shard_map/ppermute | solution.py:377
  24.6 1.0 %shard_map.62 = (f32[16,768]{1,0:T(8,128)S(1)}, f32[16,768]{1,0:T(8,128)S(1)}) custom-call(f32[16,768]{1,0:T(8,128)S(1)} %collective-permute-done.12.known, f32[16,768]{1,0:T(8,128)S(1)} %collective-permute-done.11.behind.z3, f32[16,768]{1,0:T(8,128)S(1)} %shard_map.58.e.z1, bf16[768,768]{1,0:T(8,128)(2,1)S(1)} %get-tuple-element.31.high.kt_high, ...), custom_call_target="tpu_custom_call" | custom-call | tf_op jit(solution)/shard_map/pallas_call | solution.py:30
  25.7 0.5 collective-permute-start.15
  26.2 0.7 %collective-permute-done.13.into = f32[16,768]{1,0:T(8,128)S(1)} collective-permute-done((f32[16,768]{1,0:T(8,128)S(1)}, f32[16,768]{1,0:T(8,128)S(1)}, u32[]{:S(2)}, u32[]{:S(2)}) %collective-permute-start.13) | collective-permute-done | bytes 49184 | tf_op jit(solution)/shard_map/ppermute | solution.py:377
  27.4 0.5 shard_map.63
  27.9 0.5 collective-permute-start.17
  28.4 0.7 %collective-permute-done.16.into = f32[16,768]{1,0:T(8,128)S(1)} collective-permute-done((f32[16,768]{1,0:T(8,128)S(1)}, f32[16,768]{1,0:T(8,128)S(1)}, u32[]{:S(2)}, u32[]{:S(2)}) %collective-permute-start.16) | collective-permute-done | bytes 49184 | tf_op jit(solution)/shard_map/ppermute | solution.py:377
  29.8 3.8 %collective-permute-start.20 = (f32[16,768]{1,0:T(8,128)S(1)}, f32[16,768]{1,0:T(8,128)S(1)}, u32[]{:S(2)}, u32[]{:S(2)}) collective-permute-start(f32[16,768]{1,0:T(8,128)S(1)} %get-tuple-element.41), channel_id=1, source_target_pairs={{0,4},{1,5},{2,6},{3,7},{4,0},{5,1},{6,9},{7,17},{8,2},{9,13},{10,... | collective-permute-start | bytes 147464 | tf_op jit(solution)/shard_map/ppermute | solution.py:377
  33.6 0.5 collective-permute-start.18
  34.2 7.3 %collective-permute-start.24 = (f32[16,768]{1,0:T(8,128)S(1)}, f32[16,768]{1,0:T(8,128)S(1)}, u32[]{:S(2)}, u32[]{:S(2)}) collective-permute-start(f32[16,768]{1,0:T(8,128)S(1)} %get-tuple-element.42.t), channel_id=1, source_target_pairs={{0,4},{1,5},{2,6},{3,7},{4,0},{5,1},{6,2},{7,3},{8,11},{9,13},{10,... | collective-permute-start | bytes 147464 | tf_op jit(solution)/shard_map/ppermute | solution.py:377
  41.5 0.8 %collective-permute-done.21.i3 = f32[16,768]{1,0:T(8,128)S(1)} collective-permute-done((f32[16,768]{1,0:T(8,128)S(1)}, f32[16,768]{1,0:T(8,128)S(1)}, u32[]{:S(2)}, u32[]{:S(2)}) %collective-permute-start.21) | collective-permute-done | bytes 49184 | tf_op jit(solution)/shard_map/ppermute | solution.py:377
  42.3 0.5 collective-permute-start.22
  42.8 0.6 %collective-permute-done.18.i0 = f32[16,768]{1,0:T(8,128)S(1)} collective-permute-done((f32[16,768]{1,0:T(8,128)S(1)}, f32[16,768]{1,0:T(8,128)S(1)}, u32[]{:S(2)}, u32[]{:S(2)}) %collective-permute-start.18) | collective-permute-done | bytes 49184 | tf_op jit(solution)/shard_map/ppermute | solution.py:377
  44.2 0.9 %collective-permute-done.25.mate = f32[16,768]{1,0:T(8,128)S(1)} collective-permute-done((f32[16,768]{1,0:T(8,128)S(1)}, f32[16,768]{1,0:T(8,128)S(1)}, u32[]{:S(2)}, u32[]{:S(2)}) %collective-permute-start.25) | collective-permute-done | bytes 49184 | tf_op jit(solution)/shard_map/ppermute | solution.py:390
  45.5 1.3 %shard_map.68 = bf16[4,16,1024]{2,1,0:T(8,128)(2,1)S(1)} custom-call(s32[3,64]{1,0:T(4,128)S(1)} %copy-done.2, bf16[16,384]{1,0:T(8,128)(2,1)S(1)} %shard_map.66.refs_1_, bf16[384,4096]{1,0:T(8,128)(2,1)S(1)} %get-tuple-element.43.refs_2_, bf16[384,4096]{1,0:T(8,128)(2,1)S(1)} %get-tuple-element.44.refs_3_), custom_call_target="tpu_custom_call" | custom-call | tf_op jit(solution)/shard_map/pallas_call | solution.py:30
  47.2 1.2 %shard_map.67.own = f32[4,16,1024]{2,1,0:T(8,128)S(1)} custom-call(s32[3,64]{1,0:T(4,128)S(1)} %copy-done.2, bf16[16,384]{1,0:T(8,128)(2,1)S(1)} %shard_map.66.refs_1_, bf16[384,4096]{1,0:T(8,128)(2,1)S(1)} %get-tuple-element.43.refs_2_, bf16[384,4096]{1,0:T(8,128)(2,1)S(1)} %get-tuple-element.44.refs_3_), custom_call_target="tpu_custom_call" | custom-call | tf_op jit(solution)/shard_map/pallas_call | solution.py:30
  48.5 3.5 %collective-permute-start.27 = (bf16[16,1024]{1,0:T(8,128)(2,1)S(1)}, bf16[16,1024]{1,0:T(8,128)(2,1)S(1)}, u32[]{:S(2)}, u32[]{:S(2)}) collective-permute-start(bf16[16,1024]{1,0:T(8,128)(2,1)S(1)} %get-tuple-element.46), channel_id=1, source_target_pairs={{0,8},{4,12},{8,0},{12,4},{16,24},{20,28},{24,16},{28,20},{1,9},{5... | collective-permute-start | bytes 98312 | tf_op jit(solution)/shard_map/ppermute | solution.py:196
  52.0 1.3 %collective-permute-start.28 = (bf16[16,1024]{1,0:T(8,128)(2,1)S(1)}, bf16[16,1024]{1,0:T(8,128)(2,1)S(1)}, u32[]{:S(2)}, u32[]{:S(2)}) collective-permute-start(bf16[16,1024]{1,0:T(8,128)(2,1)S(1)} %get-tuple-element.47), channel_id=1, source_target_pairs={{0,16},{4,20},{8,24},{12,28},{16,0},{20,4},{24,8},{28,12},{1,17},{... | collective-permute-start | bytes 98312 | tf_op jit(solution)/shard_map/ppermute | solution.py:196
  53.9 2.0 %collective-permute-done.28.two = bf16[16,1024]{1,0:T(8,128)(2,1)S(1)} collective-permute-done((bf16[16,1024]{1,0:T(8,128)(2,1)S(1)}, bf16[16,1024]{1,0:T(8,128)(2,1)S(1)}, u32[]{:S(2)}, u32[]{:S(2)}) %collective-permute-start.28) | collective-permute-done | bytes 32800 | tf_op jit(solution)/shard_map/ppermute | solution.py:196
  56.0 2.2 %collective-permute-done.29.three = bf16[16,1024]{1,0:T(8,128)(2,1)S(1)} collective-permute-done((bf16[16,1024]{1,0:T(8,128)(2,1)S(1)}, bf16[16,1024]{1,0:T(8,128)(2,1)S(1)}, u32[]{:S(2)}, u32[]{:S(2)}) %collective-permute-start.29) | collective-permute-done | bytes 32800 | tf_op jit(solution)/shard_map/ppermute | solution.py:196
  58.2 0.6 %shard_map.70 = f32[16,1024]{1,0:T(8,128)} custom-call(f32[16,1024]{1,0:T(8,128)S(1)} %get-tuple-element.45.keep, bf16[16,1024]{1,0:T(8,128)(2,1)S(1)} %collective-permute-done.27.one, bf16[16,1024]{1,0:T(8,128)(2,1)S(1)} %collective-permute-done.28.two, bf16[16,1024]{1,0:T(8,128)(2,1)S(1)} %collective-permute-done.29.three), custom_call_target="tpu_custom_call" | custom-call | tf_op jit(solution)/shard_map/pallas_call | solution.py:30
  (50 shorter events, 6.2 us)
Async XLA Ops:
  0.0 9.3 %copy-start = (f32[384,768]{1,0:T(8,128)S(1)}, f32[384,768]{1,0:T(8,128)}, u32[]{:S(2)}) copy-start(f32[384,768]{1,0:T(8,128)} %inv.3) | copy-start | bytes 3538948
  0.0 9.3 %collective-permute-start.4 = (f32[384,768]{1,0:T(8,128)}, f32[384,768]{1,0:T(8,128)S(1)}, u32[]{:S(2)}, u32[]{:S(2)}) collective-permute-start(f32[384,768]{1,0:T(8,128)} %refs_2_.3), channel_id=1, source_target_pairs={{0,4},{1,5},{2,6},{3,7},{4,0},{5,1},{6,2},{7,3},{8,12},{9,13},{10,... | collective-permute-start | bytes 3538952 | tf_op jit(solution)/shard_map/ppermute | solution.py:377
  0.5 8.8 %collective-permute-start.3 = (f32[384,768]{1,0:T(8,128)}, f32[384,768]{1,0:T(8,128)S(1)}, u32[]{:S(2)}, u32[]{:S(2)}) collective-permute-start(f32[384,768]{1,0:T(8,128)} %inv.3), channel_id=1, source_target_pairs={{0,4},{1,5},{2,6},{3,7},{4,0},{5,1},{6,2},{7,3},{8,12},{9,13},{10,... | collective-permute-start | bytes 3538952 | tf_op jit(solution)/shard_map/ppermute | solution.py:377
  4.6 4.8 %collective-permute-start.2 = (f32[16,384]{1,0:T(8,128)S(1)}, f32[16,384]{1,0:T(8,128)S(1)}, u32[]{:S(2)}, u32[]{:S(2)}) collective-permute-start(f32[16,384]{1,0:T(8,128)S(1)} %get-tuple-element.27.f0), channel_id=1, source_target_pairs={{0,4},{1,2},{2,1},{3,7},{4,0},{5,6},{6,5},{7,3},{8,12},{9,10},{10,... | collective-permute-start | bytes 73736 | tf_op jit(solution)/shard_map/ppermute | solution.py:377
  5.1 5.9 %collective-permute-start.1 = (f32[16,384]{1,0:T(8,128)S(1)}, f32[16,384]{1,0:T(8,128)S(1)}, u32[]{:S(2)}, u32[]{:S(2)}) collective-permute-start(f32[16,384]{1,0:T(8,128)S(1)} %get-tuple-element.27.f0), channel_id=1, source_target_pairs={{0,1},{1,0},{2,6},{3,7},{4,5},{5,4},{6,2},{7,3},{8,9},{9,8},{10,14... | collective-permute-start | bytes 73736 | tf_op jit(solution)/shard_map/ppermute | solution.py:377
  9.3 1.8 %collective-permute-start = (f32[16,384]{1,0:T(8,128)S(1)}, f32[16,384]{1,0:T(8,128)S(1)}, u32[]{:S(2)}, u32[]{:S(2)}) collective-permute-start(f32[16,384]{1,0:T(8,128)S(1)} %get-tuple-element.27.f0), channel_id=1, source_target_pairs={{0,4},{1,2},{2,3},{3,1},{4,0},{5,6},{6,7},{7,5},{8,12},{9,10},{10,... | collective-permute-start | bytes 73736 | tf_op jit(solution)/shard_map/ppermute | solution.py:377
  11.4 1.3 %collective-permute-start.5 = (f32[16,768]{1,0:T(8,128)S(1)}, f32[16,768]{1,0:T(8,128)S(1)}, u32[]{:S(2)}, u32[]{:S(2)}) collective-permute-start(f32[16,768]{1,0:T(8,128)S(1)} %shard_map.57.own), channel_id=1, source_target_pairs={{0,4},{4,0},{8,12},{12,8},{16,20},{20,16},{24,28},{28,24},{1,5},{5... | collective-permute-start | bytes 147464 | tf_op jit(solution)/shard_map/ppermute | solution.py:390
  12.7 1.3 %collective-permute-start.8 = (f32[16,768]{1,0:T(8,128)S(1)}, f32[16,768]{1,0:T(8,128)S(1)}, u32[]{:S(2)}, u32[]{:S(2)}) collective-permute-start(f32[16,768]{1,0:T(8,128)S(1)} %shard_map.58.e.z1), channel_id=1, source_target_pairs={{0,4},{1,24},{2,6},{3,7},{4,0},{5,1},{6,2},{7,3},{8,12},{9,13},{10... | collective-permute-start | bytes 147464 | tf_op jit(solution)/shard_map/ppermute | solution.py:377
  12.8 1.3 %collective-permute-start.7 = (f32[16,768]{1,0:T(8,128)S(1)}, f32[16,768]{1,0:T(8,128)S(1)}, u32[]{:S(2)}, u32[]{:S(2)}) collective-permute-start(f32[16,768]{1,0:T(8,128)S(1)} %shard_map.58.e.z1), channel_id=1, source_target_pairs={{0,4},{1,16},{2,6},{3,7},{4,0},{5,1},{6,2},{7,3},{8,12},{9,8},{10,... | collective-permute-start | bytes 147464 | tf_op jit(solution)/shard_map/ppermute | solution.py:377
  13.2 1.2 %collective-permute-start.6 = (f32[16,768]{1,0:T(8,128)S(1)}, f32[16,768]{1,0:T(8,128)S(1)}, u32[]{:S(2)}, u32[]{:S(2)}) collective-permute-start(f32[16,768]{1,0:T(8,128)S(1)} %shard_map.58.e.z1), channel_id=1, source_target_pairs={{0,4},{1,8},{2,6},{3,7},{4,0},{5,1},{6,2},{7,3},{8,12},{9,13},{10,... | collective-permute-start | bytes 147464 | tf_op jit(solution)/shard_map/ppermute | solution.py:377
  14.9 1.2 %collective-permute-start.10 = (f32[16,768]{1,0:T(8,128)S(1)}, f32[16,768]{1,0:T(8,128)S(1)}, u32[]{:S(2)}, u32[]{:S(2)}) collective-permute-start(f32[16,768]{1,0:T(8,128)S(1)} %shard_map.60.s), channel_id=1, source_target_pairs={{0,4},{1,2},{2,6},{3,7},{4,0},{5,1},{6,5},{7,3},{8,25},{9,13},{10,... | collective-permute-start | bytes 147464 | tf_op jit(solution)/shard_map/ppermute | solution.py:377
  15.0 7.8 %collective-permute-start.9 = (f32[16,768]{1,0:T(8,128)S(1)}, f32[16,768]{1,0:T(8,128)S(1)}, u32[]{:S(2)}, u32[]{:S(2)}) collective-permute-start(f32[16,768]{1,0:T(8,128)S(1)} %shard_map.60.s), channel_id=1, source_target_pairs={{0,4},{1,0},{2,6},{3,7},{4,5},{5,1},{6,2},{7,3},{8,17},{9,13},{10,... | collective-permute-start | bytes 147464 | tf_op jit(solution)/shard_map/ppermute | solution.py:377
  23.2 1.2 %collective-permute-start.12 = (f32[16,768]{1,0:T(8,128)S(1)}, f32[16,768]{1,0:T(8,128)S(1)}, u32[]{:S(2)}, u32[]{:S(2)}) collective-permute-start(f32[16,768]{1,0:T(8,128)S(1)} %shard_map.61.s), channel_id=1, source_target_pairs={{0,4},{1,5},{2,6},{3,7},{4,0},{5,1},{6,2},{7,3},{8,12},{9,13},{10,... | collective-permute-start | bytes 147464 | tf_op jit(solution)/shard_map/ppermute | solution.py:377
  23.3 1.4 %collective-permute-start.11 = (f32[16,768]{1,0:T(8,128)S(1)}, f32[16,768]{1,0:T(8,128)S(1)}, u32[]{:S(2)}, u32[]{:S(2)}) collective-permute-start(f32[16,768]{1,0:T(8,128)S(1)} %shard_map.61.s), channel_id=1, source_target_pairs={{0,4},{1,3},{2,6},{3,7},{4,0},{5,1},{6,2},{7,5},{8,12},{9,13},{10,... | collective-permute-start | bytes 147464 | tf_op jit(solution)/shard_map/ppermute | solution.py:377
  25.7 1.2 %collective-permute-start.13 = (f32[16,768]{1,0:T(8,128)S(1)}, f32[16,768]{1,0:T(8,128)S(1)}, u32[]{:S(2)}, u32[]{:S(2)}) collective-permute-start(f32[16,768]{1,0:T(8,128)S(1)} %get-tuple-element.34), channel_id=1, source_target_pairs={{0,4},{1,5},{2,6},{3,7},{4,0},{5,1},{6,2},{7,3},{8,12},{9,13},{10,... | collective-permute-start | bytes 147464 | tf_op jit(solution)/shard_map/ppermute | solution.py:377
  25.7 1.4 %collective-permute-start.15 = (f32[16,768]{1,0:T(8,128)S(1)}, f32[16,768]{1,0:T(8,128)S(1)}, u32[]{:S(2)}, u32[]{:S(2)}) collective-permute-start(f32[16,768]{1,0:T(8,128)S(1)} %get-tuple-element.35.t), channel_id=1, source_target_pairs={{0,4},{1,5},{2,6},{3,7},{4,0},{5,1},{6,2},{7,3},{8,12},{9,13},{10,... | collective-permute-start | bytes 147464 | tf_op jit(solution)/shard_map/ppermute | solution.py:377
  26.2 1.2 %collective-permute-start.14 = (f32[16,768]{1,0:T(8,128)S(1)}, f32[16,768]{1,0:T(8,128)S(1)}, u32[]{:S(2)}, u32[]{:S(2)}) collective-permute-start(f32[16,768]{1,0:T(8,128)S(1)} %get-tuple-element.35.t), channel_id=1, source_target_pairs={{0,4},{1,5},{2,6},{3,7},{4,0},{5,1},{6,2},{7,3},{8,12},{9,13},{10,... | collective-permute-start | bytes 147464 | tf_op jit(solution)/shard_map/ppermute | solution.py:377
  27.9 1.2 %collective-permute-start.16 = (f32[16,768]{1,0:T(8,128)S(1)}, f32[16,768]{1,0:T(8,128)S(1)}, u32[]{:S(2)}, u32[]{:S(2)}) collective-permute-start(f32[16,768]{1,0:T(8,128)S(1)} %get-tuple-element.38), channel_id=1, source_target_pairs={{0,4},{1,5},{2,6},{3,7},{4,0},{5,1},{6,2},{7,3},{8,12},{9,13},{10,... | collective-permute-start | bytes 147464 | tf_op jit(solution)/shard_map/ppermute | solution.py:377
  27.9 1.4 %collective-permute-start.17 = (f32[16,768]{1,0:T(8,128)S(1)}, f32[16,768]{1,0:T(8,128)S(1)}, u32[]{:S(2)}, u32[]{:S(2)}) collective-permute-start(f32[16,768]{1,0:T(8,128)S(1)} %get-tuple-element.39), channel_id=1, source_target_pairs={{0,4},{1,5},{2,6},{3,7},{4,0},{5,1},{6,2},{7,3},{8,12},{9,13},{10,... | collective-permute-start | bytes 147464 | tf_op jit(solution)/shard_map/ppermute | solution.py:377
  29.8 15.7 %copy-start.2 = (s32[3,64]{1,0:T(4,128)S(1)}, s32[3,64]{1,0:T(4,128)}, u32[]{:S(2)}) copy-start(s32[3,64]{1,0:T(4,128)} %refs_0_.7) | copy-start | bytes 2308
  29.8 12.5 %collective-permute-start.21 = (f32[16,768]{1,0:T(8,128)S(1)}, f32[16,768]{1,0:T(8,128)S(1)}, u32[]{:S(2)}, u32[]{:S(2)}) collective-permute-start(f32[16,768]{1,0:T(8,128)S(1)} %get-tuple-element.41), channel_id=1, source_target_pairs={{0,4},{1,5},{2,6},{3,7},{4,18},{5,1},{6,2},{7,24},{8,3},{9,13},{10... | collective-permute-start | bytes 147464 | tf_op jit(solution)/shard_map/ppermute | solution.py:377
  29.8 12.5 %collective-permute-start.20 = (f32[16,768]{1,0:T(8,128)S(1)}, f32[16,768]{1,0:T(8,128)S(1)}, u32[]{:S(2)}, u32[]{:S(2)}) collective-permute-start(f32[16,768]{1,0:T(8,128)S(1)} %get-tuple-element.41), channel_id=1, source_target_pairs={{0,4},{1,5},{2,6},{3,7},{4,0},{5,1},{6,9},{7,17},{8,2},{9,13},{10,... | collective-permute-start | bytes 147464 | tf_op jit(solution)/shard_map/ppermute | solution.py:377
  33.6 9.2 %collective-permute-start.19 = (f32[16,768]{1,0:T(8,128)S(1)}, f32[16,768]{1,0:T(8,128)S(1)}, u32[]{:S(2)}, u32[]{:S(2)}) collective-permute-start(f32[16,768]{1,0:T(8,128)S(1)} %get-tuple-element.41), channel_id=1, source_target_pairs={{0,4},{1,5},{2,6},{3,7},{4,0},{5,12},{6,25},{7,3},{8,1},{9,13},{10... | collective-permute-start | bytes 147464 | tf_op jit(solution)/shard_map/ppermute | solution.py:377
  33.6 9.8 %collective-permute-start.18 = (f32[16,768]{1,0:T(8,128)S(1)}, f32[16,768]{1,0:T(8,128)S(1)}, u32[]{:S(2)}, u32[]{:S(2)}) collective-permute-start(f32[16,768]{1,0:T(8,128)S(1)} %get-tuple-element.41), channel_id=1, source_target_pairs={{0,4},{1,5},{2,6},{3,7},{4,12},{5,20},{6,2},{7,3},{8,0},{9,13},{10... | collective-permute-start | bytes 147464 | tf_op jit(solution)/shard_map/ppermute | solution.py:377
  34.2 9.3 %collective-permute-start.24 = (f32[16,768]{1,0:T(8,128)S(1)}, f32[16,768]{1,0:T(8,128)S(1)}, u32[]{:S(2)}, u32[]{:S(2)}) collective-permute-start(f32[16,768]{1,0:T(8,128)S(1)} %get-tuple-element.42.t), channel_id=1, source_target_pairs={{0,4},{1,5},{2,6},{3,7},{4,0},{5,1},{6,2},{7,3},{8,11},{9,13},{10,... | collective-permute-start | bytes 147464 | tf_op jit(solution)/shard_map/ppermute | solution.py:377
  42.3 1.2 %collective-permute-start.23 = (f32[16,768]{1,0:T(8,128)S(1)}, f32[16,768]{1,0:T(8,128)S(1)}, u32[]{:S(2)}, u32[]{:S(2)}) collective-permute-start(f32[16,768]{1,0:T(8,128)S(1)} %get-tuple-element.42.t), channel_id=1, source_target_pairs={{0,4},{1,5},{2,6},{3,7},{4,0},{5,1},{6,2},{7,3},{8,10},{9,13},{10,... | collective-permute-start | bytes 147464 | tf_op jit(solution)/shard_map/ppermute | solution.py:377
  42.3 1.4 %collective-permute-start.22 = (f32[16,768]{1,0:T(8,128)S(1)}, f32[16,768]{1,0:T(8,128)S(1)}, u32[]{:S(2)}, u32[]{:S(2)}) collective-permute-start(f32[16,768]{1,0:T(8,128)S(1)} %get-tuple-element.42.t), channel_id=1, source_target_pairs={{0,4},{1,5},{2,6},{3,7},{4,0},{5,1},{6,2},{7,3},{8,9},{9,13},{10,1... | collective-permute-start | bytes 147464 | tf_op jit(solution)/shard_map/ppermute | solution.py:377
  43.8 1.3 %collective-permute-start.25 = (f32[16,768]{1,0:T(8,128)S(1)}, f32[16,768]{1,0:T(8,128)S(1)}, u32[]{:S(2)}, u32[]{:S(2)}) collective-permute-start(f32[16,768]{1,0:T(8,128)S(1)} %shard_map.65.own), channel_id=1, source_target_pairs={{0,4},{4,0},{8,12},{12,8},{16,20},{20,16},{24,28},{28,24},{1,5},{5... | collective-permute-start | bytes 147464 | tf_op jit(solution)/shard_map/ppermute | solution.py:390
  46.8 1.7 %collective-permute-start.26 = (bf16[4,16,1024]{2,1,0:T(8,128)(2,1)S(1)}, bf16[4,16,1024]{2,1,0:T(8,128)(2,1)S(1)}, u32[]{:S(2)}, u32[]{:S(2)}) collective-permute-start(bf16[4,16,1024]{2,1,0:T(8,128)(2,1)S(1)} %shard_map.68), channel_id=1, source_target_pairs={{0,4},{4,0},{8,12},{12,8},{16,20},{20,16},{24,28},{28,24},{1,5},{5... | collective-permute-start | bytes 393224 | tf_op jit(solution)/shard_map/ppermute | solution.py:196
  48.5 5.4 %collective-permute-start.27 = (bf16[16,1024]{1,0:T(8,128)(2,1)S(1)}, bf16[16,1024]{1,0:T(8,128)(2,1)S(1)}, u32[]{:S(2)}, u32[]{:S(2)}) collective-permute-start(bf16[16,1024]{1,0:T(8,128)(2,1)S(1)} %get-tuple-element.46), channel_id=1, source_target_pairs={{0,8},{4,12},{8,0},{12,4},{16,24},{20,28},{24,16},{28,20},{1,9},{5... | collective-permute-start | bytes 98312 | tf_op jit(solution)/shard_map/ppermute | solution.py:196
  52.0 3.9 %collective-permute-start.28 = (bf16[16,1024]{1,0:T(8,128)(2,1)S(1)}, bf16[16,1024]{1,0:T(8,128)(2,1)S(1)}, u32[]{:S(2)}, u32[]{:S(2)}) collective-permute-start(bf16[16,1024]{1,0:T(8,128)(2,1)S(1)} %get-tuple-element.47), channel_id=1, source_target_pairs={{0,16},{4,20},{8,24},{12,28},{16,0},{20,4},{24,8},{28,12},{1,17},{... | collective-permute-start | bytes 98312 | tf_op jit(solution)/shard_map/ppermute | solution.py:196
  53.3 4.8 %collective-permute-start.29 = (bf16[16,1024]{1,0:T(8,128)(2,1)S(1)}, bf16[16,1024]{1,0:T(8,128)(2,1)S(1)}, u32[]{:S(2)}, u32[]{:S(2)}) collective-permute-start(bf16[16,1024]{1,0:T(8,128)(2,1)S(1)} %get-tuple-element.48), channel_id=1, source_target_pairs={{0,24},{4,28},{8,16},{12,20},{16,8},{20,12},{24,0},{28,4},{1,25},{... | collective-permute-start | bytes 98312 | tf_op jit(solution)/shard_map/ppermute | solution.py:196
  (1 other events, 9.3 us)
where the time goes:
time: 58.9 us; the launch traced here: 58.8 us
  starting transfers between devices  26.1 us (44%)
  waiting for transfers between devices  21.5 us (37%)
  Pallas kernels  11 us (19%)
    ppermute x24, starting transfers between devices, permute(): return lax.ppermute(value, AXES, sorted(to.items()))  20.2 us
    ppermute x24, waiting for transfers between devices, permute(): return lax.ppermute(value, AXES, sorted(to.items()))  14.8 us
    pallas_call x16, Pallas kernels, call(): pl.pallas_call(kernel, out_shape=outs, in_specs=specs or [VMEM] * len(ope...  11 us
    ppermute x4, starting transfers between devices, move(): return lax.ppermute(value, 'aux', [(i, to(i)) for i in range(members)])  5.5 us
    ppermute x4, waiting for transfers between devices, move(): return lax.ppermute(value, 'aux', [(i, to(i)) for i in range(members)])  4.57 us
    ppermute x2, waiting for transfers between devices, swap(): lax.ppermute(value, 'aux', [(i, i ^ 1) for i in range(2 * SOLVE_BLOCKS)])  2.13 us
  transfers between devices with their start and end apart: 30, of which 22 were waited for; matrix products, arithmetic and copies ran while one was open for 0% of the time, Pallas kernels for 9%

commit v1 on v0

--- a/solution.py
+++ b/solution.py
@@ -224,19 +224,14 @@
     return both[:rows] + both[rows:]
 
 
-def prepare_first(*refs):
-    here = (block_of() == 0) | (lax.axis_index("pair") > 0)
-    prepare(here, *refs)
-
-
-def prepare_later(*refs):
-    prepare(lax.axis_index("pair") == 0, *refs)
-
-
-def prepare(here, inv0, inv1, fac0, fac1, k_high, k_low, kt_high, kt_low, lhs, rhs):
+def leads_block():
+    return (block_of() > 0) & (side_of() == 0)
+
+
+def prepare_first(inv0, inv1, fac0, fac1, k_high, k_low, kt_high, kt_low, lhs, rhs):
     height = inv0.shape[0]
 
-    @pl.when(here & (block_of() > 0) & (side_of() == 0))
+    @pl.when(leads_block())
     def _():
         for n, (inv, fac) in enumerate(((inv0, fac0), (inv1, fac1))):
             rows = [slice((3 * n + r) * height, (3 * n + r + 1) * height) for r in range(3)]
@@ -244,15 +239,26 @@
             lhs[rows[0], :], lhs[rows[1], :], lhs[rows[2], :] = high, low, high
             high, low = high_low(fac[...])
             rhs[rows[0], :], rhs[rows[1], :], rhs[rows[2], :] = high, high, low
-        depth = 3 * height
-        halves = (
-            (slice(0, height), slice(0, depth)),
-            (slice(height, 2 * height), slice(0, 2 * depth)),
-        )
-        for part, used in halves:
-            product = lax.dot_general(lhs[used, part], rhs[used, :], TN, preferred_element_type=F32)
-            k_high[part, :], k_low[part, :] = high_low(product)
-            kt_high[:, part], kt_low[:, part] = high_low(product.T)
+
+    @pl.when(leads_block() & (lax.axis_index("pair") > 0))
+    def _():
+        multiply_up(lhs, rhs, k_high, k_low, kt_high, kt_low)
+
+
+def prepare_later(*refs):
+    pl.when(leads_block() & (lax.axis_index("pair") == 0))(lambda: multiply_up(*refs))
+
+
+def multiply_up(lhs, rhs, k_high, k_low, kt_high, kt_low):
+    depth, size = lhs.shape[0] // 2, lhs.shape[1]
+    parts = (
+        (slice(0, size // 2), slice(0, depth)),
+        (slice(size // 2, size), slice(0, 2 * depth)),
+    )
+    for part, used in parts:
+        product = lax.dot_general(lhs[used, part], rhs[used, :], TN, preferred_element_type=F32)
+        k_high[part, :], k_low[part, :] = high_low(product)
+        kt_high[:, part], kt_low[:, part] = high_low(product.T)
 
 
 def begin(f0, f1, f2, f3, inv, after, out):
@@ -391,6 +397,13 @@
 
     panel = struct((count, size))
     square = struct((size, size), BF16)
+    halves = (diag_inv, swap(diag_inv), factor, swap(factor))
+
+    stacked = struct((3 * size, size), BF16)
+    k_high, k_low, kt_high, kt_low, *pairs = call(
+        prepare_first, [square] * 4 + [stacked] * 2, *halves, limit=24
+    )
+    at_zero = call(prepare_later, [square] * 4, *pairs, limit=24)
     home = [1, 1, 1, 2]
     gathered = []
     for route in ("far", "other", "middle"):
@@ -403,14 +416,6 @@
                 loop = [device((k, plane), c) for plane in ring[route]]
                 to.update(zip(loop, loop[1:] + loop[:1]))
         gathered.append(permute(partial_fit, to))
-    halves = (diag_inv, permute(diag_inv, {}), factor, permute(factor, {}))
-
-    def prepared(kernel):
-        scratch = [pltpu.VMEM((3 * size, size), BF16)] * 2
-        return call(kernel, [square] * 4, *halves, limit=32, scratch=scratch)
-
-    k_high, k_low, kt_high, kt_low = prepared(prepare_first)
-    at_zero = prepared(prepare_later)
     e = call(begin, panel, partial_fit, *gathered, diag_inv, k_high)
     e = call(both, panel, e, swap(e))
     reach = [

time: 58.9 us -> 58.9 us (level)
    ppermute x24 -> x22, starting transfers between devices: 20.2 us -> 19.7 us  [permute(): return lax.ppermute(value, AXES, sorted(to.items()))]
    ppermute x24 -> x22, waiting for transfers between devices: 14.8 us -> 14.8 us  [permute(): return lax.ppermute(value, AXES, sorted(to.items()))]
    ppermute x2 -> x4, waiting for transfers between devices: 2.13 us -> 2.14 us  [swap(): lax.ppermute(value, 'aux', [(i, i ^ 1) for i in range(2 * SOLVE_BLOCKS)])]
where the time goes in v1:
time: 58.9 us; the launch traced here: 58.8 us
  starting transfers between devices  26.1 us (44%)
  waiting for transfers between devices  21.5 us (37%)
  Pallas kernels  11 us (19%)
    ppermute x22, starting transfers between devices, permute(): return lax.ppermute(value, AXES, sorted(to.items()))  19.7 us
    ppermute x22, waiting for transfers between devices, permute(): return lax.ppermute(value, AXES, sorted(to.items()))  14.8 us
    pallas_call x16, Pallas kernels, call(): pl.pallas_call(kernel, out_shape=outs, in_specs=specs or [VMEM] * len(ope...  11 us
    ppermute x4, starting transfers between devices, move(): return lax.ppermute(value, 'aux', [(i, to(i)) for i in range(members)])  5.5 us
    ppermute x4, waiting for transfers between devices, move(): return lax.ppermute(value, 'aux', [(i, to(i)) for i in range(members)])  4.57 us
    ppermute x4, waiting for transfers between devices, swap(): lax.ppermute(value, 'aux', [(i, i ^ 1) for i in range(2 * SOLVE_BLOCKS)])  2.14 us
  transfers between devices with their start and end apart: 30, of which 22 were waited for; matrix products, arithmetic and copies ran while one was open for 0% of the time, Pallas kernels for 9%

profile of v1, /device:TPU:0, one launch (start us, length us, event | category | flops | bytes accessed | tf_op | source)
XLA Modules:
  0.0 58.8 jit_solution(14419488630060508345)
XLA Ops:
  0.0 0.5 collective-permute-start.4
  0.6 4.0 %shard_map.55 = (bf16[384,4096]{1,0:T(8,128)(2,1)S(1)}, bf16[384,4096]{1,0:T(8,128)(2,1)S(1)}, f32[16,384]{1,0:T(8,128)S(1)}) custom-call(s32[3,64]{1,0:T(4,128)} %refs_0_.3, bf16[16,8192]{1,0:T(8,128)(2,1)} %densities_in.1, bf16[384,8192]{1,0:T(8,128)(2,1)} %integrals.1), custom_call_target="tpu_custom_call" | custom-call | tf_op jit(solution)/shard_map/pallas_call | solution.py:30
  4.6 0.6 collective-permute-start.2
  5.1 4.1 %collective-permute-start.1 = (f32[16,384]{1,0:T(8,128)S(1)}, f32[16,384]{1,0:T(8,128)S(1)}, u32[]{:S(2)}, u32[]{:S(2)}) collective-permute-start(f32[16,384]{1,0:T(8,128)S(1)} %get-tuple-element.29.f0), channel_id=1, source_target_pairs={{0,1},{1,0},{2,6},{3,7},{4,5},{5,4},{6,2},{7,3},{8,9},{9,8},{10,14... | collective-permute-start | bytes 73736 | tf_op jit(solution)/shard_map/ppermute | solution.py:383
  9.4 1.7 %collective-permute-done.1.f2 = f32[16,384]{1,0:T(8,128)S(1)} collective-permute-done((f32[16,384]{1,0:T(8,128)S(1)}, f32[16,384]{1,0:T(8,128)S(1)}, u32[]{:S(2)}, u32[]{:S(2)}) %collective-permute-start.1) | collective-permute-done | bytes 24608 | tf_op jit(solution)/shard_map/ppermute | solution.py:383
  11.4 1.2 %collective-permute-done.5.mate = f32[16,768]{1,0:T(8,128)S(1)} collective-permute-done((f32[16,768]{1,0:T(8,128)S(1)}, f32[16,768]{1,0:T(8,128)S(1)}, u32[]{:S(2)}, u32[]{:S(2)}) %collective-permute-start.5) | collective-permute-done | bytes 49184 | tf_op jit(solution)/shard_map/ppermute | solution.py:396
  13.3 0.6 %collective-permute-done.8.three = f32[16,768]{1,0:T(8,128)S(1)} collective-permute-done((f32[16,768]{1,0:T(8,128)S(1)}, f32[16,768]{1,0:T(8,128)S(1)}, u32[]{:S(2)}, u32[]{:S(2)}) %collective-permute-start.8) | collective-permute-done | bytes 49184 | tf_op jit(solution)/shard_map/ppermute | solution.py:383
  15.0 0.5 collective-permute-start.9
  15.5 0.7 %collective-permute-done.10.second.z2 = f32[16,768]{1,0:T(8,128)S(1)} collective-permute-done((f32[16,768]{1,0:T(8,128)S(1)}, f32[16,768]{1,0:T(8,128)S(1)}, u32[]{:S(2)}, u32[]{:S(2)}) %collective-permute-start.10) | collective-permute-done | bytes 49184 | tf_op jit(solution)/shard_map/ppermute | solution.py:383
  16.2 6.6 %collective-permute-done.9.first.z0 = f32[16,768]{1,0:T(8,128)S(1)} collective-permute-done((f32[16,768]{1,0:T(8,128)S(1)}, f32[16,768]{1,0:T(8,128)S(1)}, u32[]{:S(2)}, u32[]{:S(2)}) %collective-permute-start.9) | collective-permute-done | bytes 49184 | tf_op jit(solution)/shard_map/ppermute | solution.py:383
  23.3 0.5 collective-permute-start.11
  23.8 0.7 %collective-permute-done.12.known = f32[16,768]{1,0:T(8,128)S(1)} collective-permute-done((f32[16,768]{1,0:T(8,128)S(1)}, f32[16,768]{1,0:T(8,128)S(1)}, u32[]{:S(2)}, u32[]{:S(2)}) %collective-permute-start.12) | collective-permute-done | bytes 49184 | tf_op jit(solution)/shard_map/ppermute | solution.py:383
  24.6 1.0 %shard_map.62 = (f32[16,768]{1,0:T(8,128)S(1)}, f32[16,768]{1,0:T(8,128)S(1)}) custom-call(f32[16,768]{1,0:T(8,128)S(1)} %collective-permute-done.12.known, f32[16,768]{1,0:T(8,128)S(1)} %collective-permute-done.11.behind.z3, f32[16,768]{1,0:T(8,128)S(1)} %shard_map.58.e.z1, bf16[768,768]{1,0:T(8,128)(2,1)S(1)} %get-tuple-element.35.high.kt_high, ...), custom_call_target="tpu_custom_call" | custom-call | tf_op jit(solution)/shard_map/pallas_call | solution.py:30
  25.7 0.5 collective-permute-start.15
  26.2 0.7 %collective-permute-done.13.into = f32[16,768]{1,0:T(8,128)S(1)} collective-permute-done((f32[16,768]{1,0:T(8,128)S(1)}, f32[16,768]{1,0:T(8,128)S(1)}, u32[]{:S(2)}, u32[]{:S(2)}) %collective-permute-start.13) | collective-permute-done | bytes 49184 | tf_op jit(solution)/shard_map/ppermute | solution.py:383
  27.4 0.5 shard_map.63
  27.9 0.5 collective-permute-start.17
  28.4 0.7 %collective-permute-done.16.into = f32[16,768]{1,0:T(8,128)S(1)} collective-permute-done((f32[16,768]{1,0:T(8,128)S(1)}, f32[16,768]{1,0:T(8,128)S(1)}, u32[]{:S(2)}, u32[]{:S(2)}) %collective-permute-start.16) | collective-permute-done | bytes 49184 | tf_op jit(solution)/shard_map/ppermute | solution.py:383
  29.8 3.8 %collective-permute-start.20 = (f32[16,768]{1,0:T(8,128)S(1)}, f32[16,768]{1,0:T(8,128)S(1)}, u32[]{:S(2)}, u32[]{:S(2)}) collective-permute-start(f32[16,768]{1,0:T(8,128)S(1)} %get-tuple-element.45), channel_id=1, source_target_pairs={{0,4},{1,5},{2,6},{3,7},{4,0},{5,1},{6,9},{7,17},{8,2},{9,13},{10,... | collective-permute-start | bytes 147464 | tf_op jit(solution)/shard_map/ppermute | solution.py:383
  33.6 0.5 collective-permute-start.18
  34.2 7.3 %collective-permute-start.24 = (f32[16,768]{1,0:T(8,128)S(1)}, f32[16,768]{1,0:T(8,128)S(1)}, u32[]{:S(2)}, u32[]{:S(2)}) collective-permute-start(f32[16,768]{1,0:T(8,128)S(1)} %get-tuple-element.46.t), channel_id=1, source_target_pairs={{0,4},{1,5},{2,6},{3,7},{4,0},{5,1},{6,2},{7,3},{8,11},{9,13},{10,... | collective-permute-start | bytes 147464 | tf_op jit(solution)/shard_map/ppermute | solution.py:383
  41.5 0.8 %collective-permute-done.21.i3 = f32[16,768]{1,0:T(8,128)S(1)} collective-permute-done((f32[16,768]{1,0:T(8,128)S(1)}, f32[16,768]{1,0:T(8,128)S(1)}, u32[]{:S(2)}, u32[]{:S(2)}) %collective-permute-start.21) | collective-permute-done | bytes 49184 | tf_op jit(solution)/shard_map/ppermute | solution.py:383
  42.3 0.5 collective-permute-start.22
  42.8 0.6 %collective-permute-done.18.i0 = f32[16,768]{1,0:T(8,128)S(1)} collective-permute-done((f32[16,768]{1,0:T(8,128)S(1)}, f32[16,768]{1,0:T(8,128)S(1)}, u32[]{:S(2)}, u32[]{:S(2)}) %collective-permute-start.18) | collective-permute-done | bytes 49184 | tf_op jit(solution)/shard_map/ppermute | solution.py:383
  44.2 0.9 %collective-permute-done.25.mate = f32[16,768]{1,0:T(8,128)S(1)} collective-permute-done((f32[16,768]{1,0:T(8,128)S(1)}, f32[16,768]{1,0:T(8,128)S(1)}, u32[]{:S(2)}, u32[]{:S(2)}) %collective-permute-start.25) | collective-permute-done | bytes 49184 | tf_op jit(solution)/shard_map/ppermute | solution.py:396
  45.5 1.3 %shard_map.68 = bf16[4,16,1024]{2,1,0:T(8,128)(2,1)S(1)} custom-call(s32[3,64]{1,0:T(4,128)S(1)} %copy-done.2, bf16[16,384]{1,0:T(8,128)(2,1)S(1)} %shard_map.66.refs_1_, bf16[384,4096]{1,0:T(8,128)(2,1)S(1)} %get-tuple-element.47.refs_2_, bf16[384,4096]{1,0:T(8,128)(2,1)S(1)} %get-tuple-element.48.refs_3_), custom_call_target="tpu_custom_call" | custom-call | tf_op jit(solution)/shard_map/pallas_call | solution.py:30
  47.2 1.2 %shard_map.67.own = f32[4,16,1024]{2,1,0:T(8,128)S(1)} custom-call(s32[3,64]{1,0:T(4,128)S(1)} %copy-done.2, bf16[16,384]{1,0:T(8,128)(2,1)S(1)} %shard_map.66.refs_1_, bf16[384,4096]{1,0:T(8,128)(2,1)S(1)} %get-tuple-element.47.refs_2_, bf16[384,4096]{1,0:T(8,128)(2,1)S(1)} %get-tuple-element.48.refs_3_), custom_call_target="tpu_custom_call" | custom-call | tf_op jit(solution)/shard_map/pallas_call | solution.py:30
  48.5 3.5 %collective-permute-start.27 = (bf16[16,1024]{1,0:T(8,128)(2,1)S(1)}, bf16[16,1024]{1,0:T(8,128)(2,1)S(1)}, u32[]{:S(2)}, u32[]{:S(2)}) collective-permute-start(bf16[16,1024]{1,0:T(8,128)(2,1)S(1)} %get-tuple-element.50), channel_id=1, source_target_pairs={{0,8},{4,12},{8,0},{12,4},{16,24},{20,28},{24,16},{28,20},{1,9},{5... | collective-permute-start | bytes 98312 | tf_op jit(solution)/shard_map/ppermute | solution.py:196
  52.0 1.3 %collective-permute-start.28 = (bf16[16,1024]{1,0:T(8,128)(2,1)S(1)}, bf16[16,1024]{1,0:T(8,128)(2,1)S(1)}, u32[]{:S(2)}, u32[]{:S(2)}) collective-permute-start(bf16[16,1024]{1,0:T(8,128)(2,1)S(1)} %get-tuple-element.51), channel_id=1, source_target_pairs={{0,16},{4,20},{8,24},{12,28},{16,0},{20,4},{24,8},{28,12},{1,17},{... | collective-permute-start | bytes 98312 | tf_op jit(solution)/shard_map/ppermute | solution.py:196
  53.9 2.0 %collective-permute-done.28.two = bf16[16,1024]{1,0:T(8,128)(2,1)S(1)} collective-permute-done((bf16[16,1024]{1,0:T(8,128)(2,1)S(1)}, bf16[16,1024]{1,0:T(8,128)(2,1)S(1)}, u32[]{:S(2)}, u32[]{:S(2)}) %collective-permute-start.28) | collective-permute-done | bytes 32800 | tf_op jit(solution)/shard_map/ppermute | solution.py:196
  56.0 2.2 %collective-permute-done.29.three = bf16[16,1024]{1,0:T(8,128)(2,1)S(1)} collective-permute-done((bf16[16,1024]{1,0:T(8,128)(2,1)S(1)}, bf16[16,1024]{1,0:T(8,128)(2,1)S(1)}, u32[]{:S(2)}, u32[]{:S(2)}) %collective-permute-start.29) | collective-permute-done | bytes 32800 | tf_op jit(solution)/shard_map/ppermute | solution.py:196
  58.2 0.6 %shard_map.70 = f32[16,1024]{1,0:T(8,128)} custom-call(f32[16,1024]{1,0:T(8,128)S(1)} %get-tuple-element.49.keep, bf16[16,1024]{1,0:T(8,128)(2,1)S(1)} %collective-permute-done.27.one, bf16[16,1024]{1,0:T(8,128)(2,1)S(1)} %collective-permute-done.28.two, bf16[16,1024]{1,0:T(8,128)(2,1)S(1)} %collective-permute-done.29.three), custom_call_target="tpu_custom_call" | custom-call | tf_op jit(solution)/shard_map/pallas_call | solution.py:30
  (50 shorter events, 6.2 us)
Async XLA Ops:
  0.0 9.3 %copy-start = (f32[384,768]{1,0:T(8,128)S(1)}, f32[384,768]{1,0:T(8,128)}, u32[]{:S(2)}) copy-start(f32[384,768]{1,0:T(8,128)} %inv.3) | copy-start | bytes 3538948
  0.0 9.3 %collective-permute-start.4 = (f32[384,768]{1,0:T(8,128)}, f32[384,768]{1,0:T(8,128)S(1)}, u32[]{:S(2)}, u32[]{:S(2)}) collective-permute-start(f32[384,768]{1,0:T(8,128)} %fac0.1), channel_id=1, source_target_pairs={{0,4},{4,0},{8,12},{12,8},{16,20},{20,16},{24,28},{28,24},{1,5},{5... | collective-permute-start | bytes 3538952 | tf_op jit(solution)/shard_map/ppermute | solution.py:396
  0.5 8.8 %collective-permute-start.3 = (f32[384,768]{1,0:T(8,128)}, f32[384,768]{1,0:T(8,128)S(1)}, u32[]{:S(2)}, u32[]{:S(2)}) collective-permute-start(f32[384,768]{1,0:T(8,128)} %inv.3), channel_id=1, source_target_pairs={{0,4},{4,0},{8,12},{12,8},{16,20},{20,16},{24,28},{28,24},{1,5},{5... | collective-permute-start | bytes 3538952 | tf_op jit(solution)/shard_map/ppermute | solution.py:396
  4.6 4.8 %collective-permute-start.2 = (f32[16,384]{1,0:T(8,128)S(1)}, f32[16,384]{1,0:T(8,128)S(1)}, u32[]{:S(2)}, u32[]{:S(2)}) collective-permute-start(f32[16,384]{1,0:T(8,128)S(1)} %get-tuple-element.29.f0), channel_id=1, source_target_pairs={{0,4},{1,2},{2,1},{3,7},{4,0},{5,6},{6,5},{7,3},{8,12},{9,10},{10,... | collective-permute-start | bytes 73736 | tf_op jit(solution)/shard_map/ppermute | solution.py:383
  5.1 5.9 %collective-permute-start.1 = (f32[16,384]{1,0:T(8,128)S(1)}, f32[16,384]{1,0:T(8,128)S(1)}, u32[]{:S(2)}, u32[]{:S(2)}) collective-permute-start(f32[16,384]{1,0:T(8,128)S(1)} %get-tuple-element.29.f0), channel_id=1, source_target_pairs={{0,1},{1,0},{2,6},{3,7},{4,5},{5,4},{6,2},{7,3},{8,9},{9,8},{10,14... | collective-permute-start | bytes 73736 | tf_op jit(solution)/shard_map/ppermute | solution.py:383
  9.3 1.8 %collective-permute-start = (f32[16,384]{1,0:T(8,128)S(1)}, f32[16,384]{1,0:T(8,128)S(1)}, u32[]{:S(2)}, u32[]{:S(2)}) collective-permute-start(f32[16,384]{1,0:T(8,128)S(1)} %get-tuple-element.29.f0), channel_id=1, source_target_pairs={{0,4},{1,2},{2,3},{3,1},{4,0},{5,6},{6,7},{7,5},{8,12},{9,10},{10,... | collective-permute-start | bytes 73736 | tf_op jit(solution)/shard_map/ppermute | solution.py:383
  11.4 1.3 %collective-permute-start.5 = (f32[16,768]{1,0:T(8,128)S(1)}, f32[16,768]{1,0:T(8,128)S(1)}, u32[]{:S(2)}, u32[]{:S(2)}) collective-permute-start(f32[16,768]{1,0:T(8,128)S(1)} %shard_map.57.own), channel_id=1, source_target_pairs={{0,4},{4,0},{8,12},{12,8},{16,20},{20,16},{24,28},{28,24},{1,5},{5... | collective-permute-start | bytes 147464 | tf_op jit(solution)/shard_map/ppermute | solution.py:396
  12.7 1.3 %collective-permute-start.8 = (f32[16,768]{1,0:T(8,128)S(1)}, f32[16,768]{1,0:T(8,128)S(1)}, u32[]{:S(2)}, u32[]{:S(2)}) collective-permute-start(f32[16,768]{1,0:T(8,128)S(1)} %shard_map.58.e.z1), channel_id=1, source_target_pairs={{0,4},{1,24},{2,6},{3,7},{4,0},{5,1},{6,2},{7,3},{8,12},{9,13},{10... | collective-permute-start | bytes 147464 | tf_op jit(solution)/shard_map/ppermute | solution.py:383
  12.8 1.3 %collective-permute-start.7 = (f32[16,768]{1,0:T(8,128)S(1)}, f32[16,768]{1,0:T(8,128)S(1)}, u32[]{:S(2)}, u32[]{:S(2)}) collective-permute-start(f32[16,768]{1,0:T(8,128)S(1)} %shard_map.58.e.z1), channel_id=1, source_target_pairs={{0,4},{1,16},{2,6},{3,7},{4,0},{5,1},{6,2},{7,3},{8,12},{9,8},{10,... | collective-permute-start | bytes 147464 | tf_op jit(solution)/shard_map/ppermute | solution.py:383
  13.2 1.2 %collective-permute-start.6 = (f32[16,768]{1,0:T(8,128)S(1)}, f32[16,768]{1,0:T(8,128)S(1)}, u32[]{:S(2)}, u32[]{:S(2)}) collective-permute-start(f32[16,768]{1,0:T(8,128)S(1)} %shard_map.58.e.z1), channel_id=1, source_target_pairs={{0,4},{1,8},{2,6},{3,7},{4,0},{5,1},{6,2},{7,3},{8,12},{9,13},{10,... | collective-permute-start | bytes 147464 | tf_op jit(solution)/shard_map/ppermute | solution.py:383
  14.9 1.2 %collective-permute-start.10 = (f32[16,768]{1,0:T(8,128)S(1)}, f32[16,768]{1,0:T(8,128)S(1)}, u32[]{:S(2)}, u32[]{:S(2)}) collective-permute-start(f32[16,768]{1,0:T(8,128)S(1)} %shard_map.60.s), channel_id=1, source_target_pairs={{0,4},{1,2},{2,6},{3,7},{4,0},{5,1},{6,5},{7,3},{8,25},{9,13},{10,... | collective-permute-start | bytes 147464 | tf_op jit(solution)/shard_map/ppermute | solution.py:383
  15.0 7.8 %collective-permute-start.9 = (f32[16,768]{1,0:T(8,128)S(1)}, f32[16,768]{1,0:T(8,128)S(1)}, u32[]{:S(2)}, u32[]{:S(2)}) collective-permute-start(f32[16,768]{1,0:T(8,128)S(1)} %shard_map.60.s), channel_id=1, source_target_pairs={{0,4},{1,0},{2,6},{3,7},{4,5},{5,1},{6,2},{7,3},{8,17},{9,13},{10,... | collective-permute-start | bytes 147464 | tf_op jit(solution)/shard_map/ppermute | solution.py:383
  23.2 1.2 %collective-permute-start.12 = (f32[16,768]{1,0:T(8,128)S(1)}, f32[16,768]{1,0:T(8,128)S(1)}, u32[]{:S(2)}, u32[]{:S(2)}) collective-permute-start(f32[16,768]{1,0:T(8,128)S(1)} %shard_map.61.s), channel_id=1, source_target_pairs={{0,4},{1,5},{2,6},{3,7},{4,0},{5,1},{6,2},{7,3},{8,12},{9,13},{10,... | collective-permute-start | bytes 147464 | tf_op jit(solution)/shard_map/ppermute | solution.py:383
  23.3 1.4 %collective-permute-start.11 = (f32[16,768]{1,0:T(8,128)S(1)}, f32[16,768]{1,0:T(8,128)S(1)}, u32[]{:S(2)}, u32[]{:S(2)}) collective-permute-start(f32[16,768]{1,0:T(8,128)S(1)} %shard_map.61.s), channel_id=1, source_target_pairs={{0,4},{1,3},{2,6},{3,7},{4,0},{5,1},{6,2},{7,5},{8,12},{9,13},{10,... | collective-permute-start | bytes 147464 | tf_op jit(solution)/shard_map/ppermute | solution.py:383
  25.7 1.2 %collective-permute-start.13 = (f32[16,768]{1,0:T(8,128)S(1)}, f32[16,768]{1,0:T(8,128)S(1)}, u32[]{:S(2)}, u32[]{:S(2)}) collective-permute-start(f32[16,768]{1,0:T(8,128)S(1)} %get-tuple-element.38), channel_id=1, source_target_pairs={{0,4},{1,5},{2,6},{3,7},{4,0},{5,1},{6,2},{7,3},{8,12},{9,13},{10,... | collective-permute-start | bytes 147464 | tf_op jit(solution)/shard_map/ppermute | solution.py:383
  25.7 1.4 %collective-permute-start.15 = (f32[16,768]{1,0:T(8,128)S(1)}, f32[16,768]{1,0:T(8,128)S(1)}, u32[]{:S(2)}, u32[]{:S(2)}) collective-permute-start(f32[16,768]{1,0:T(8,128)S(1)} %get-tuple-element.39.t), channel_id=1, source_target_pairs={{0,4},{1,5},{2,6},{3,7},{4,0},{5,1},{6,2},{7,3},{8,12},{9,13},{10,... | collective-permute-start | bytes 147464 | tf_op jit(solution)/shard_map/ppermute | solution.py:383
  26.2 1.2 %collective-permute-start.14 = (f32[16,768]{1,0:T(8,128)S(1)}, f32[16,768]{1,0:T(8,128)S(1)}, u32[]{:S(2)}, u32[]{:S(2)}) collective-permute-start(f32[16,768]{1,0:T(8,128)S(1)} %get-tuple-element.39.t), channel_id=1, source_target_pairs={{0,4},{1,5},{2,6},{3,7},{4,0},{5,1},{6,2},{7,3},{8,12},{9,13},{10,... | collective-permute-start | bytes 147464 | tf_op jit(solution)/shard_map/ppermute | solution.py:383
  27.9 1.2 %collective-permute-start.16 = (f32[16,768]{1,0:T(8,128)S(1)}, f32[16,768]{1,0:T(8,128)S(1)}, u32[]{:S(2)}, u32[]{:S(2)}) collective-permute-start(f32[16,768]{1,0:T(8,128)S(1)} %get-tuple-element.42), channel_id=1, source_target_pairs={{0,4},{1,5},{2,6},{3,7},{4,0},{5,1},{6,2},{7,3},{8,12},{9,13},{10,... | collective-permute-start | bytes 147464 | tf_op jit(solution)/shard_map/ppermute | solution.py:383
  27.9 1.4 %collective-permute-start.17 = (f32[16,768]{1,0:T(8,128)S(1)}, f32[16,768]{1,0:T(8,128)S(1)}, u32[]{:S(2)}, u32[]{:S(2)}) collective-permute-start(f32[16,768]{1,0:T(8,128)S(1)} %get-tuple-element.43), channel_id=1, source_target_pairs={{0,4},{1,5},{2,6},{3,7},{4,0},{5,1},{6,2},{7,3},{8,12},{9,13},{10,... | collective-permute-start | bytes 147464 | tf_op jit(solution)/shard_map/ppermute | solution.py:383
  29.8 15.7 %copy-start.2 = (s32[3,64]{1,0:T(4,128)S(1)}, s32[3,64]{1,0:T(4,128)}, u32[]{:S(2)}) copy-start(s32[3,64]{1,0:T(4,128)} %refs_0_.3) | copy-start | bytes 2308
  29.8 12.5 %collective-permute-start.21 = (f32[16,768]{1,0:T(8,128)S(1)}, f32[16,768]{1,0:T(8,128)S(1)}, u32[]{:S(2)}, u32[]{:S(2)}) collective-permute-start(f32[16,768]{1,0:T(8,128)S(1)} %get-tuple-element.45), channel_id=1, source_target_pairs={{0,4},{1,5},{2,6},{3,7},{4,18},{5,1},{6,2},{7,24},{8,3},{9,13},{10... | collective-permute-start | bytes 147464 | tf_op jit(solution)/shard_map/ppermute | solution.py:383
  29.8 12.5 %collective-permute-start.20 = (f32[16,768]{1,0:T(8,128)S(1)}, f32[16,768]{1,0:T(8,128)S(1)}, u32[]{:S(2)}, u32[]{:S(2)}) collective-permute-start(f32[16,768]{1,0:T(8,128)S(1)} %get-tuple-element.45), channel_id=1, source_target_pairs={{0,4},{1,5},{2,6},{3,7},{4,0},{5,1},{6,9},{7,17},{8,2},{9,13},{10,... | collective-permute-start | bytes 147464 | tf_op jit(solution)/shard_map/ppermute | solution.py:383
  33.6 9.2 %collective-permute-start.19 = (f32[16,768]{1,0:T(8,128)S(1)}, f32[16,768]{1,0:T(8,128)S(1)}, u32[]{:S(2)}, u32[]{:S(2)}) collective-permute-start(f32[16,768]{1,0:T(8,128)S(1)} %get-tuple-element.45), channel_id=1, source_target_pairs={{0,4},{1,5},{2,6},{3,7},{4,0},{5,12},{6,25},{7,3},{8,1},{9,13},{10... | collective-permute-start | bytes 147464 | tf_op jit(solution)/shard_map/ppermute | solution.py:383
  33.6 9.8 %collective-permute-start.18 = (f32[16,768]{1,0:T(8,128)S(1)}, f32[16,768]{1,0:T(8,128)S(1)}, u32[]{:S(2)}, u32[]{:S(2)}) collective-permute-start(f32[16,768]{1,0:T(8,128)S(1)} %get-tuple-element.45), channel_id=1, source_target_pairs={{0,4},{1,5},{2,6},{3,7},{4,12},{5,20},{6,2},{7,3},{8,0},{9,13},{10... | collective-permute-start | bytes 147464 | tf_op jit(solution)/shard_map/ppermute | solution.py:383
  34.2 9.3 %collective-permute-start.24 = (f32[16,768]{1,0:T(8,128)S(1)}, f32[16,768]{1,0:T(8,128)S(1)}, u32[]{:S(2)}, u32[]{:S(2)}) collective-permute-start(f32[16,768]{1,0:T(8,128)S(1)} %get-tuple-element.46.t), channel_id=1, source_target_pairs={{0,4},{1,5},{2,6},{3,7},{4,0},{5,1},{6,2},{7,3},{8,11},{9,13},{10,... | collective-permute-start | bytes 147464 | tf_op jit(solution)/shard_map/ppermute | solution.py:383
  42.3 1.2 %collective-permute-start.23 = (f32[16,768]{1,0:T(8,128)S(1)}, f32[16,768]{1,0:T(8,128)S(1)}, u32[]{:S(2)}, u32[]{:S(2)}) collective-permute-start(f32[16,768]{1,0:T(8,128)S(1)} %get-tuple-element.46.t), channel_id=1, source_target_pairs={{0,4},{1,5},{2,6},{3,7},{4,0},{5,1},{6,2},{7,3},{8,10},{9,13},{10,... | collective-permute-start | bytes 147464 | tf_op jit(solution)/shard_map/ppermute | solution.py:383
  42.3 1.4 %collective-permute-start.22 = (f32[16,768]{1,0:T(8,128)S(1)}, f32[16,768]{1,0:T(8,128)S(1)}, u32[]{:S(2)}, u32[]{:S(2)}) collective-permute-start(f32[16,768]{1,0:T(8,128)S(1)} %get-tuple-element.46.t), channel_id=1, source_target_pairs={{0,4},{1,5},{2,6},{3,7},{4,0},{5,1},{6,2},{7,3},{8,9},{9,13},{10,1... | collective-permute-start | bytes 147464 | tf_op jit(solution)/shard_map/ppermute | solution.py:383
  43.8 1.3 %collective-permute-start.25 = (f32[16,768]{1,0:T(8,128)S(1)}, f32[16,768]{1,0:T(8,128)S(1)}, u32[]{:S(2)}, u32[]{:S(2)}) collective-permute-start(f32[16,768]{1,0:T(8,128)S(1)} %shard_map.65.own), channel_id=1, source_target_pairs={{0,4},{4,0},{8,12},{12,8},{16,20},{20,16},{24,28},{28,24},{1,5},{5... | collective-permute-start | bytes 147464 | tf_op jit(solution)/shard_map/ppermute | solution.py:396
  46.8 1.7 %collective-permute-start.26 = (bf16[4,16,1024]{2,1,0:T(8,128)(2,1)S(1)}, bf16[4,16,1024]{2,1,0:T(8,128)(2,1)S(1)}, u32[]{:S(2)}, u32[]{:S(2)}) collective-permute-start(bf16[4,16,1024]{2,1,0:T(8,128)(2,1)S(1)} %shard_map.68), channel_id=1, source_target_pairs={{0,4},{4,0},{8,12},{12,8},{16,20},{20,16},{24,28},{28,24},{1,5},{5... | collective-permute-start | bytes 393224 | tf_op jit(solution)/shard_map/ppermute | solution.py:196
  48.5 5.4 %collective-permute-start.27 = (bf16[16,1024]{1,0:T(8,128)(2,1)S(1)}, bf16[16,1024]{1,0:T(8,128)(2,1)S(1)}, u32[]{:S(2)}, u32[]{:S(2)}) collective-permute-start(bf16[16,1024]{1,0:T(8,128)(2,1)S(1)} %get-tuple-element.50), channel_id=1, source_target_pairs={{0,8},{4,12},{8,0},{12,4},{16,24},{20,28},{24,16},{28,20},{1,9},{5... | collective-permute-start | bytes 98312 | tf_op jit(solution)/shard_map/ppermute | solution.py:196
  52.0 3.9 %collective-permute-start.28 = (bf16[16,1024]{1,0:T(8,128)(2,1)S(1)}, bf16[16,1024]{1,0:T(8,128)(2,1)S(1)}, u32[]{:S(2)}, u32[]{:S(2)}) collective-permute-start(bf16[16,1024]{1,0:T(8,128)(2,1)S(1)} %get-tuple-element.51), channel_id=1, source_target_pairs={{0,16},{4,20},{8,24},{12,28},{16,0},{20,4},{24,8},{28,12},{1,17},{... | collective-permute-start | bytes 98312 | tf_op jit(solution)/shard_map/ppermute | solution.py:196
  53.3 4.8 %collective-permute-start.29 = (bf16[16,1024]{1,0:T(8,128)(2,1)S(1)}, bf16[16,1024]{1,0:T(8,128)(2,1)S(1)}, u32[]{:S(2)}, u32[]{:S(2)}) collective-permute-start(bf16[16,1024]{1,0:T(8,128)(2,1)S(1)} %get-tuple-element.52), channel_id=1, source_target_pairs={{0,24},{4,28},{8,16},{12,20},{16,8},{20,12},{24,0},{28,4},{1,25},{... | collective-permute-start | bytes 98312 | tf_op jit(solution)/shard_map/ppermute | solution.py:196
  (1 other events, 9.3 us)

commit v2 on v0

--- a/solution.py
+++ b/solution.py
@@ -225,8 +225,7 @@
 
 
 def prepare_first(*refs):
-    here = (block_of() == 0) | (lax.axis_index("pair") > 0)
-    prepare(here, *refs)
+    prepare(lax.axis_index("pair") > 0, *refs)
 
 
 def prepare_later(*refs):
@@ -236,7 +235,7 @@
 def prepare(here, inv0, inv1, fac0, fac1, k_high, k_low, kt_high, kt_low, lhs, rhs):
     height = inv0.shape[0]
 
-    @pl.when(here & (block_of() > 0) & (side_of() == 0))
+    @pl.when(here & (lax.axis_index("pair") < block_of()) & (side_of() == 0))
     def _():
         for n, (inv, fac) in enumerate(((inv0, fac0), (inv1, fac1))):
             rows = [slice((3 * n + r) * height, (3 * n + r + 1) * height) for r in range(3)]
@@ -391,6 +390,14 @@
 
     panel = struct((count, size))
     square = struct((size, size), BF16)
+    halves = (diag_inv, swap(diag_inv), factor, swap(factor))
+
+    def prepared(kernel):
+        scratch = [pltpu.VMEM((3 * size, size), BF16)] * 2
+        return call(kernel, [square] * 4, *halves, limit=32, scratch=scratch)
+
+    k_high, k_low, kt_high, kt_low = prepared(prepare_first)
+    at_zero = prepared(prepare_later)
     home = [1, 1, 1, 2]
     gathered = []
     for route in ("far", "other", "middle"):
@@ -403,14 +410,6 @@
                 loop = [device((k, plane), c) for plane in ring[route]]
                 to.update(zip(loop, loop[1:] + loop[:1]))
         gathered.append(permute(partial_fit, to))
-    halves = (diag_inv, permute(diag_inv, {}), factor, permute(factor, {}))
-
-    def prepared(kernel):
-        scratch = [pltpu.VMEM((3 * size, size), BF16)] * 2
-        return call(kernel, [square] * 4, *halves, limit=32, scratch=scratch)
-
-    k_high, k_low, kt_high, kt_low = prepared(prepare_first)
-    at_zero = prepared(prepare_later)
     e = call(begin, panel, partial_fit, *gathered, diag_inv, k_high)
     e = call(both, panel, e, swap(e))
     reach = [

time: 58.9 us -> 58.9 us (level)
    ppermute x24 -> x22, starting transfers between devices: 20.2 us -> 19.7 us  [permute(): return lax.ppermute(value, AXES, sorted(to.items()))]
    ppermute x2 -> x4, waiting for transfers between devices: 2.13 us -> 2.14 us  [swap(): lax.ppermute(value, 'aux', [(i, i ^ 1) for i in range(2 * SOLVE_BLOCKS)])]
    ppermute x24 -> x22, waiting for transfers between devices: 14.8 us -> 14.8 us  [permute(): return lax.ppermute(value, AXES, sorted(to.items()))]
where the time goes in v2:
time: 58.9 us; the launch traced here: 58.8 us
  starting transfers between devices  26.1 us (44%)
  waiting for transfers between devices  21.5 us (37%)
  Pallas kernels  11 us (19%)
    ppermute x22, starting transfers between devices, permute(): return lax.ppermute(value, AXES, sorted(to.items()))  19.7 us
    ppermute x22, waiting for transfers between devices, permute(): return lax.ppermute(value, AXES, sorted(to.items()))  14.8 us
    pallas_call x16, Pallas kernels, call(): pl.pallas_call(kernel, out_shape=outs, in_specs=specs or [VMEM] * len(ope...  11 us
    ppermute x4, starting transfers between devices, move(): return lax.ppermute(value, 'aux', [(i, to(i)) for i in range(members)])  5.5 us
    ppermute x4, waiting for transfers between devices, move(): return lax.ppermute(value, 'aux', [(i, to(i)) for i in range(members)])  4.57 us
    ppermute x4, waiting for transfers between devices, swap(): lax.ppermute(value, 'aux', [(i, i ^ 1) for i in range(2 * SOLVE_BLOCKS)])  2.14 us
  transfers between devices with their start and end apart: 30, of which 22 were waited for; matrix products, arithmetic and copies ran while one was open for 0% of the time, Pallas kernels for 9%

profile of v2, /device:TPU:0, one launch (start us, length us, event | category | flops | bytes accessed | tf_op | source)
XLA Modules:
  0.0 58.8 jit_solution(1687397535361223124)
XLA Ops:
  0.0 0.5 collective-permute-start.4
  0.6 4.0 %shard_map.55 = (bf16[384,4096]{1,0:T(8,128)(2,1)S(1)}, bf16[384,4096]{1,0:T(8,128)(2,1)S(1)}, f32[16,384]{1,0:T(8,128)S(1)}) custom-call(s32[3,64]{1,0:T(4,128)} %refs_0_.7, bf16[16,8192]{1,0:T(8,128)(2,1)} %densities_in.1, bf16[384,8192]{1,0:T(8,128)(2,1)} %integrals.1), custom_call_target="tpu_custom_call" | custom-call | tf_op jit(solution)/shard_map/pallas_call | solution.py:30
  4.6 0.6 collective-permute-start.2
  5.1 4.1 %collective-permute-start.1 = (f32[16,384]{1,0:T(8,128)S(1)}, f32[16,384]{1,0:T(8,128)S(1)}, u32[]{:S(2)}, u32[]{:S(2)}) collective-permute-start(f32[16,384]{1,0:T(8,128)S(1)} %get-tuple-element.27.f0), channel_id=1, source_target_pairs={{0,1},{1,0},{2,6},{3,7},{4,5},{5,4},{6,2},{7,3},{8,9},{9,8},{10,14... | collective-permute-start | bytes 73736 | tf_op jit(solution)/shard_map/ppermute | solution.py:376
  9.4 1.7 %collective-permute-done.1.f2 = f32[16,384]{1,0:T(8,128)S(1)} collective-permute-done((f32[16,384]{1,0:T(8,128)S(1)}, f32[16,384]{1,0:T(8,128)S(1)}, u32[]{:S(2)}, u32[]{:S(2)}) %collective-permute-start.1) | collective-permute-done | bytes 24608 | tf_op jit(solution)/shard_map/ppermute | solution.py:376
  11.4 1.2 %collective-permute-done.5.mate = f32[16,768]{1,0:T(8,128)S(1)} collective-permute-done((f32[16,768]{1,0:T(8,128)S(1)}, f32[16,768]{1,0:T(8,128)S(1)}, u32[]{:S(2)}, u32[]{:S(2)}) %collective-permute-start.5) | collective-permute-done | bytes 49184 | tf_op jit(solution)/shard_map/ppermute | solution.py:389
  13.3 0.6 %collective-permute-done.8.three = f32[16,768]{1,0:T(8,128)S(1)} collective-permute-done((f32[16,768]{1,0:T(8,128)S(1)}, f32[16,768]{1,0:T(8,128)S(1)}, u32[]{:S(2)}, u32[]{:S(2)}) %collective-permute-start.8) | collective-permute-done | bytes 49184 | tf_op jit(solution)/shard_map/ppermute | solution.py:376
  15.0 0.5 collective-permute-start.9
  15.5 0.7 %collective-permute-done.10.second.z2 = f32[16,768]{1,0:T(8,128)S(1)} collective-permute-done((f32[16,768]{1,0:T(8,128)S(1)}, f32[16,768]{1,0:T(8,128)S(1)}, u32[]{:S(2)}, u32[]{:S(2)}) %collective-permute-start.10) | collective-permute-done | bytes 49184 | tf_op jit(solution)/shard_map/ppermute | solution.py:376
  16.2 6.6 %collective-permute-done.9.first.z0 = f32[16,768]{1,0:T(8,128)S(1)} collective-permute-done((f32[16,768]{1,0:T(8,128)S(1)}, f32[16,768]{1,0:T(8,128)S(1)}, u32[]{:S(2)}, u32[]{:S(2)}) %collective-permute-start.9) | collective-permute-done | bytes 49184 | tf_op jit(solution)/shard_map/ppermute | solution.py:376
  23.3 0.5 collective-permute-start.11
  23.8 0.7 %collective-permute-done.12.known = f32[16,768]{1,0:T(8,128)S(1)} collective-permute-done((f32[16,768]{1,0:T(8,128)S(1)}, f32[16,768]{1,0:T(8,128)S(1)}, u32[]{:S(2)}, u32[]{:S(2)}) %collective-permute-start.12) | collective-permute-done | bytes 49184 | tf_op jit(solution)/shard_map/ppermute | solution.py:376
  24.6 1.0 %shard_map.62 = (f32[16,768]{1,0:T(8,128)S(1)}, f32[16,768]{1,0:T(8,128)S(1)}) custom-call(f32[16,768]{1,0:T(8,128)S(1)} %collective-permute-done.12.known, f32[16,768]{1,0:T(8,128)S(1)} %collective-permute-done.11.behind.z3, f32[16,768]{1,0:T(8,128)S(1)} %shard_map.58.e.z1, bf16[768,768]{1,0:T(8,128)(2,1)S(1)} %get-tuple-element.31.high.kt_high, ...), custom_call_target="tpu_custom_call" | custom-call | tf_op jit(solution)/shard_map/pallas_call | solution.py:30
  25.7 0.5 collective-permute-start.15
  26.2 0.7 %collective-permute-done.13.into = f32[16,768]{1,0:T(8,128)S(1)} collective-permute-done((f32[16,768]{1,0:T(8,128)S(1)}, f32[16,768]{1,0:T(8,128)S(1)}, u32[]{:S(2)}, u32[]{:S(2)}) %collective-permute-start.13) | collective-permute-done | bytes 49184 | tf_op jit(solution)/shard_map/ppermute | solution.py:376
  27.4 0.5 shard_map.63
  27.9 0.5 collective-permute-start.17
  28.4 0.7 %collective-permute-done.16.into = f32[16,768]{1,0:T(8,128)S(1)} collective-permute-done((f32[16,768]{1,0:T(8,128)S(1)}, f32[16,768]{1,0:T(8,128)S(1)}, u32[]{:S(2)}, u32[]{:S(2)}) %collective-permute-start.16) | collective-permute-done | bytes 49184 | tf_op jit(solution)/shard_map/ppermute | solution.py:376
  29.8 3.8 %collective-permute-start.20 = (f32[16,768]{1,0:T(8,128)S(1)}, f32[16,768]{1,0:T(8,128)S(1)}, u32[]{:S(2)}, u32[]{:S(2)}) collective-permute-start(f32[16,768]{1,0:T(8,128)S(1)} %get-tuple-element.41), channel_id=1, source_target_pairs={{0,4},{1,5},{2,6},{3,7},{4,0},{5,1},{6,9},{7,17},{8,2},{9,13},{10,... | collective-permute-start | bytes 147464 | tf_op jit(solution)/shard_map/ppermute | solution.py:376
  33.6 0.5 collective-permute-start.18
  34.2 7.3 %collective-permute-start.24 = (f32[16,768]{1,0:T(8,128)S(1)}, f32[16,768]{1,0:T(8,128)S(1)}, u32[]{:S(2)}, u32[]{:S(2)}) collective-permute-start(f32[16,768]{1,0:T(8,128)S(1)} %get-tuple-element.42.t), channel_id=1, source_target_pairs={{0,4},{1,5},{2,6},{3,7},{4,0},{5,1},{6,2},{7,3},{8,11},{9,13},{10,... | collective-permute-start | bytes 147464 | tf_op jit(solution)/shard_map/ppermute | solution.py:376
  41.5 0.8 %collective-permute-done.21.i3 = f32[16,768]{1,0:T(8,128)S(1)} collective-permute-done((f32[16,768]{1,0:T(8,128)S(1)}, f32[16,768]{1,0:T(8,128)S(1)}, u32[]{:S(2)}, u32[]{:S(2)}) %collective-permute-start.21) | collective-permute-done | bytes 49184 | tf_op jit(solution)/shard_map/ppermute | solution.py:376
  42.3 0.5 collective-permute-start.22
  42.8 0.6 %collective-permute-done.18.i0 = f32[16,768]{1,0:T(8,128)S(1)} collective-permute-done((f32[16,768]{1,0:T(8,128)S(1)}, f32[16,768]{1,0:T(8,128)S(1)}, u32[]{:S(2)}, u32[]{:S(2)}) %collective-permute-start.18) | collective-permute-done | bytes 49184 | tf_op jit(solution)/shard_map/ppermute | solution.py:376
  44.2 0.9 %collective-permute-done.25.mate = f32[16,768]{1,0:T(8,128)S(1)} collective-permute-done((f32[16,768]{1,0:T(8,128)S(1)}, f32[16,768]{1,0:T(8,128)S(1)}, u32[]{:S(2)}, u32[]{:S(2)}) %collective-permute-start.25) | collective-permute-done | bytes 49184 | tf_op jit(solution)/shard_map/ppermute | solution.py:389
  45.5 1.3 %shard_map.68 = bf16[4,16,1024]{2,1,0:T(8,128)(2,1)S(1)} custom-call(s32[3,64]{1,0:T(4,128)S(1)} %copy-done.2, bf16[16,384]{1,0:T(8,128)(2,1)S(1)} %shard_map.66.refs_1_, bf16[384,4096]{1,0:T(8,128)(2,1)S(1)} %get-tuple-element.43.refs_2_, bf16[384,4096]{1,0:T(8,128)(2,1)S(1)} %get-tuple-element.44.refs_3_), custom_call_target="tpu_custom_call" | custom-call | tf_op jit(solution)/shard_map/pallas_call | solution.py:30
  47.2 1.2 %shard_map.67.own = f32[4,16,1024]{2,1,0:T(8,128)S(1)} custom-call(s32[3,64]{1,0:T(4,128)S(1)} %copy-done.2, bf16[16,384]{1,0:T(8,128)(2,1)S(1)} %shard_map.66.refs_1_, bf16[384,4096]{1,0:T(8,128)(2,1)S(1)} %get-tuple-element.43.refs_2_, bf16[384,4096]{1,0:T(8,128)(2,1)S(1)} %get-tuple-element.44.refs_3_), custom_call_target="tpu_custom_call" | custom-call | tf_op jit(solution)/shard_map/pallas_call | solution.py:30
  48.5 3.5 %collective-permute-start.27 = (bf16[16,1024]{1,0:T(8,128)(2,1)S(1)}, bf16[16,1024]{1,0:T(8,128)(2,1)S(1)}, u32[]{:S(2)}, u32[]{:S(2)}) collective-permute-start(bf16[16,1024]{1,0:T(8,128)(2,1)S(1)} %get-tuple-element.46), channel_id=1, source_target_pairs={{0,8},{4,12},{8,0},{12,4},{16,24},{20,28},{24,16},{28,20},{1,9},{5... | collective-permute-start | bytes 98312 | tf_op jit(solution)/shard_map/ppermute | solution.py:196
  52.0 1.3 %collective-permute-start.28 = (bf16[16,1024]{1,0:T(8,128)(2,1)S(1)}, bf16[16,1024]{1,0:T(8,128)(2,1)S(1)}, u32[]{:S(2)}, u32[]{:S(2)}) collective-permute-start(bf16[16,1024]{1,0:T(8,128)(2,1)S(1)} %get-tuple-element.47), channel_id=1, source_target_pairs={{0,16},{4,20},{8,24},{12,28},{16,0},{20,4},{24,8},{28,12},{1,17},{... | collective-permute-start | bytes 98312 | tf_op jit(solution)/shard_map/ppermute | solution.py:196
  53.9 2.0 %collective-permute-done.28.two = bf16[16,1024]{1,0:T(8,128)(2,1)S(1)} collective-permute-done((bf16[16,1024]{1,0:T(8,128)(2,1)S(1)}, bf16[16,1024]{1,0:T(8,128)(2,1)S(1)}, u32[]{:S(2)}, u32[]{:S(2)}) %collective-permute-start.28) | collective-permute-done | bytes 32800 | tf_op jit(solution)/shard_map/ppermute | solution.py:196
  56.0 2.2 %collective-permute-done.29.three = bf16[16,1024]{1,0:T(8,128)(2,1)S(1)} collective-permute-done((bf16[16,1024]{1,0:T(8,128)(2,1)S(1)}, bf16[16,1024]{1,0:T(8,128)(2,1)S(1)}, u32[]{:S(2)}, u32[]{:S(2)}) %collective-permute-start.29) | collective-permute-done | bytes 32800 | tf_op jit(solution)/shard_map/ppermute | solution.py:196
  58.2 0.6 %shard_map.70 = f32[16,1024]{1,0:T(8,128)} custom-call(f32[16,1024]{1,0:T(8,128)S(1)} %get-tuple-element.45.keep, bf16[16,1024]{1,0:T(8,128)(2,1)S(1)} %collective-permute-done.27.one, bf16[16,1024]{1,0:T(8,128)(2,1)S(1)} %collective-permute-done.28.two, bf16[16,1024]{1,0:T(8,128)(2,1)S(1)} %collective-permute-done.29.three), custom_call_target="tpu_custom_call" | custom-call | tf_op jit(solution)/shard_map/pallas_call | solution.py:30
  (50 shorter events, 6.2 us)
Async XLA Ops:
  0.0 9.3 %copy-start = (f32[384,768]{1,0:T(8,128)S(1)}, f32[384,768]{1,0:T(8,128)}, u32[]{:S(2)}) copy-start(f32[384,768]{1,0:T(8,128)} %inv.3) | copy-start | bytes 3538948
  0.0 9.3 %collective-permute-start.4 = (f32[384,768]{1,0:T(8,128)}, f32[384,768]{1,0:T(8,128)S(1)}, u32[]{:S(2)}, u32[]{:S(2)}) collective-permute-start(f32[384,768]{1,0:T(8,128)} %refs_2_.3), channel_id=1, source_target_pairs={{0,4},{4,0},{8,12},{12,8},{16,20},{20,16},{24,28},{28,24},{1,5},{5... | collective-permute-start | bytes 3538952 | tf_op jit(solution)/shard_map/ppermute | solution.py:389
  0.5 8.8 %collective-permute-start.3 = (f32[384,768]{1,0:T(8,128)}, f32[384,768]{1,0:T(8,128)S(1)}, u32[]{:S(2)}, u32[]{:S(2)}) collective-permute-start(f32[384,768]{1,0:T(8,128)} %inv.3), channel_id=1, source_target_pairs={{0,4},{4,0},{8,12},{12,8},{16,20},{20,16},{24,28},{28,24},{1,5},{5... | collective-permute-start | bytes 3538952 | tf_op jit(solution)/shard_map/ppermute | solution.py:389
  4.6 4.8 %collective-permute-start.2 = (f32[16,384]{1,0:T(8,128)S(1)}, f32[16,384]{1,0:T(8,128)S(1)}, u32[]{:S(2)}, u32[]{:S(2)}) collective-permute-start(f32[16,384]{1,0:T(8,128)S(1)} %get-tuple-element.27.f0), channel_id=1, source_target_pairs={{0,4},{1,2},{2,1},{3,7},{4,0},{5,6},{6,5},{7,3},{8,12},{9,10},{10,... | collective-permute-start | bytes 73736 | tf_op jit(solution)/shard_map/ppermute | solution.py:376
  5.1 5.9 %collective-permute-start.1 = (f32[16,384]{1,0:T(8,128)S(1)}, f32[16,384]{1,0:T(8,128)S(1)}, u32[]{:S(2)}, u32[]{:S(2)}) collective-permute-start(f32[16,384]{1,0:T(8,128)S(1)} %get-tuple-element.27.f0), channel_id=1, source_target_pairs={{0,1},{1,0},{2,6},{3,7},{4,5},{5,4},{6,2},{7,3},{8,9},{9,8},{10,14... | collective-permute-start | bytes 73736 | tf_op jit(solution)/shard_map/ppermute | solution.py:376
  9.3 1.8 %collective-permute-start = (f32[16,384]{1,0:T(8,128)S(1)}, f32[16,384]{1,0:T(8,128)S(1)}, u32[]{:S(2)}, u32[]{:S(2)}) collective-permute-start(f32[16,384]{1,0:T(8,128)S(1)} %get-tuple-element.27.f0), channel_id=1, source_target_pairs={{0,4},{1,2},{2,3},{3,1},{4,0},{5,6},{6,7},{7,5},{8,12},{9,10},{10,... | collective-permute-start | bytes 73736 | tf_op jit(solution)/shard_map/ppermute | solution.py:376
  11.4 1.3 %collective-permute-start.5 = (f32[16,768]{1,0:T(8,128)S(1)}, f32[16,768]{1,0:T(8,128)S(1)}, u32[]{:S(2)}, u32[]{:S(2)}) collective-permute-start(f32[16,768]{1,0:T(8,128)S(1)} %shard_map.57.own), channel_id=1, source_target_pairs={{0,4},{4,0},{8,12},{12,8},{16,20},{20,16},{24,28},{28,24},{1,5},{5... | collective-permute-start | bytes 147464 | tf_op jit(solution)/shard_map/ppermute | solution.py:389
  12.7 1.3 %collective-permute-start.8 = (f32[16,768]{1,0:T(8,128)S(1)}, f32[16,768]{1,0:T(8,128)S(1)}, u32[]{:S(2)}, u32[]{:S(2)}) collective-permute-start(f32[16,768]{1,0:T(8,128)S(1)} %shard_map.58.e.z1), channel_id=1, source_target_pairs={{0,4},{1,24},{2,6},{3,7},{4,0},{5,1},{6,2},{7,3},{8,12},{9,13},{10... | collective-permute-start | bytes 147464 | tf_op jit(solution)/shard_map/ppermute | solution.py:376
  12.8 1.3 %collective-permute-start.7 = (f32[16,768]{1,0:T(8,128)S(1)}, f32[16,768]{1,0:T(8,128)S(1)}, u32[]{:S(2)}, u32[]{:S(2)}) collective-permute-start(f32[16,768]{1,0:T(8,128)S(1)} %shard_map.58.e.z1), channel_id=1, source_target_pairs={{0,4},{1,16},{2,6},{3,7},{4,0},{5,1},{6,2},{7,3},{8,12},{9,8},{10,... | collective-permute-start | bytes 147464 | tf_op jit(solution)/shard_map/ppermute | solution.py:376
  13.2 1.2 %collective-permute-start.6 = (f32[16,768]{1,0:T(8,128)S(1)}, f32[16,768]{1,0:T(8,128)S(1)}, u32[]{:S(2)}, u32[]{:S(2)}) collective-permute-start(f32[16,768]{1,0:T(8,128)S(1)} %shard_map.58.e.z1), channel_id=1, source_target_pairs={{0,4},{1,8},{2,6},{3,7},{4,0},{5,1},{6,2},{7,3},{8,12},{9,13},{10,... | collective-permute-start | bytes 147464 | tf_op jit(solution)/shard_map/ppermute | solution.py:376
  14.9 1.2 %collective-permute-start.10 = (f32[16,768]{1,0:T(8,128)S(1)}, f32[16,768]{1,0:T(8,128)S(1)}, u32[]{:S(2)}, u32[]{:S(2)}) collective-permute-start(f32[16,768]{1,0:T(8,128)S(1)} %shard_map.60.s), channel_id=1, source_target_pairs={{0,4},{1,2},{2,6},{3,7},{4,0},{5,1},{6,5},{7,3},{8,25},{9,13},{10,... | collective-permute-start | bytes 147464 | tf_op jit(solution)/shard_map/ppermute | solution.py:376
  15.0 7.8 %collective-permute-start.9 = (f32[16,768]{1,0:T(8,128)S(1)}, f32[16,768]{1,0:T(8,128)S(1)}, u32[]{:S(2)}, u32[]{:S(2)}) collective-permute-start(f32[16,768]{1,0:T(8,128)S(1)} %shard_map.60.s), channel_id=1, source_target_pairs={{0,4},{1,0},{2,6},{3,7},{4,5},{5,1},{6,2},{7,3},{8,17},{9,13},{10,... | collective-permute-start | bytes 147464 | tf_op jit(solution)/shard_map/ppermute | solution.py:376
  23.2 1.2 %collective-permute-start.12 = (f32[16,768]{1,0:T(8,128)S(1)}, f32[16,768]{1,0:T(8,128)S(1)}, u32[]{:S(2)}, u32[]{:S(2)}) collective-permute-start(f32[16,768]{1,0:T(8,128)S(1)} %shard_map.61.s), channel_id=1, source_target_pairs={{0,4},{1,5},{2,6},{3,7},{4,0},{5,1},{6,2},{7,3},{8,12},{9,13},{10,... | collective-permute-start | bytes 147464 | tf_op jit(solution)/shard_map/ppermute | solution.py:376
  23.3 1.4 %collective-permute-start.11 = (f32[16,768]{1,0:T(8,128)S(1)}, f32[16,768]{1,0:T(8,128)S(1)}, u32[]{:S(2)}, u32[]{:S(2)}) collective-permute-start(f32[16,768]{1,0:T(8,128)S(1)} %shard_map.61.s), channel_id=1, source_target_pairs={{0,4},{1,3},{2,6},{3,7},{4,0},{5,1},{6,2},{7,5},{8,12},{9,13},{10,... | collective-permute-start | bytes 147464 | tf_op jit(solution)/shard_map/ppermute | solution.py:376
  25.7 1.2 %collective-permute-start.13 = (f32[16,768]{1,0:T(8,128)S(1)}, f32[16,768]{1,0:T(8,128)S(1)}, u32[]{:S(2)}, u32[]{:S(2)}) collective-permute-start(f32[16,768]{1,0:T(8,128)S(1)} %get-tuple-element.34), channel_id=1, source_target_pairs={{0,4},{1,5},{2,6},{3,7},{4,0},{5,1},{6,2},{7,3},{8,12},{9,13},{10,... | collective-permute-start | bytes 147464 | tf_op jit(solution)/shard_map/ppermute | solution.py:376
  25.7 1.4 %collective-permute-start.15 = (f32[16,768]{1,0:T(8,128)S(1)}, f32[16,768]{1,0:T(8,128)S(1)}, u32[]{:S(2)}, u32[]{:S(2)}) collective-permute-start(f32[16,768]{1,0:T(8,128)S(1)} %get-tuple-element.35.t), channel_id=1, source_target_pairs={{0,4},{1,5},{2,6},{3,7},{4,0},{5,1},{6,2},{7,3},{8,12},{9,13},{10,... | collective-permute-start | bytes 147464 | tf_op jit(solution)/shard_map/ppermute | solution.py:376
  26.2 1.2 %collective-permute-start.14 = (f32[16,768]{1,0:T(8,128)S(1)}, f32[16,768]{1,0:T(8,128)S(1)}, u32[]{:S(2)}, u32[]{:S(2)}) collective-permute-start(f32[16,768]{1,0:T(8,128)S(1)} %get-tuple-element.35.t), channel_id=1, source_target_pairs={{0,4},{1,5},{2,6},{3,7},{4,0},{5,1},{6,2},{7,3},{8,12},{9,13},{10,... | collective-permute-start | bytes 147464 | tf_op jit(solution)/shard_map/ppermute | solution.py:376
  27.9 1.2 %collective-permute-start.16 = (f32[16,768]{1,0:T(8,128)S(1)}, f32[16,768]{1,0:T(8,128)S(1)}, u32[]{:S(2)}, u32[]{:S(2)}) collective-permute-start(f32[16,768]{1,0:T(8,128)S(1)} %get-tuple-element.38), channel_id=1, source_target_pairs={{0,4},{1,5},{2,6},{3,7},{4,0},{5,1},{6,2},{7,3},{8,12},{9,13},{10,... | collective-permute-start | bytes 147464 | tf_op jit(solution)/shard_map/ppermute | solution.py:376
  27.9 1.4 %collective-permute-start.17 = (f32[16,768]{1,0:T(8,128)S(1)}, f32[16,768]{1,0:T(8,128)S(1)}, u32[]{:S(2)}, u32[]{:S(2)}) collective-permute-start(f32[16,768]{1,0:T(8,128)S(1)} %get-tuple-element.39), channel_id=1, source_target_pairs={{0,4},{1,5},{2,6},{3,7},{4,0},{5,1},{6,2},{7,3},{8,12},{9,13},{10,... | collective-permute-start | bytes 147464 | tf_op jit(solution)/shard_map/ppermute | solution.py:376
  29.8 15.7 %copy-start.2 = (s32[3,64]{1,0:T(4,128)S(1)}, s32[3,64]{1,0:T(4,128)}, u32[]{:S(2)}) copy-start(s32[3,64]{1,0:T(4,128)} %refs_0_.7) | copy-start | bytes 2308
  29.8 12.5 %collective-permute-start.21 = (f32[16,768]{1,0:T(8,128)S(1)}, f32[16,768]{1,0:T(8,128)S(1)}, u32[]{:S(2)}, u32[]{:S(2)}) collective-permute-start(f32[16,768]{1,0:T(8,128)S(1)} %get-tuple-element.41), channel_id=1, source_target_pairs={{0,4},{1,5},{2,6},{3,7},{4,18},{5,1},{6,2},{7,24},{8,3},{9,13},{10... | collective-permute-start | bytes 147464 | tf_op jit(solution)/shard_map/ppermute | solution.py:376
  29.8 12.5 %collective-permute-start.20 = (f32[16,768]{1,0:T(8,128)S(1)}, f32[16,768]{1,0:T(8,128)S(1)}, u32[]{:S(2)}, u32[]{:S(2)}) collective-permute-start(f32[16,768]{1,0:T(8,128)S(1)} %get-tuple-element.41), channel_id=1, source_target_pairs={{0,4},{1,5},{2,6},{3,7},{4,0},{5,1},{6,9},{7,17},{8,2},{9,13},{10,... | collective-permute-start | bytes 147464 | tf_op jit(solution)/shard_map/ppermute | solution.py:376
  33.6 9.2 %collective-permute-start.19 = (f32[16,768]{1,0:T(8,128)S(1)}, f32[16,768]{1,0:T(8,128)S(1)}, u32[]{:S(2)}, u32[]{:S(2)}) collective-permute-start(f32[16,768]{1,0:T(8,128)S(1)} %get-tuple-element.41), channel_id=1, source_target_pairs={{0,4},{1,5},{2,6},{3,7},{4,0},{5,12},{6,25},{7,3},{8,1},{9,13},{10... | collective-permute-start | bytes 147464 | tf_op jit(solution)/shard_map/ppermute | solution.py:376
  33.6 9.8 %collective-permute-start.18 = (f32[16,768]{1,0:T(8,128)S(1)}, f32[16,768]{1,0:T(8,128)S(1)}, u32[]{:S(2)}, u32[]{:S(2)}) collective-permute-start(f32[16,768]{1,0:T(8,128)S(1)} %get-tuple-element.41), channel_id=1, source_target_pairs={{0,4},{1,5},{2,6},{3,7},{4,12},{5,20},{6,2},{7,3},{8,0},{9,13},{10... | collective-permute-start | bytes 147464 | tf_op jit(solution)/shard_map/ppermute | solution.py:376
  34.2 9.3 %collective-permute-start.24 = (f32[16,768]{1,0:T(8,128)S(1)}, f32[16,768]{1,0:T(8,128)S(1)}, u32[]{:S(2)}, u32[]{:S(2)}) collective-permute-start(f32[16,768]{1,0:T(8,128)S(1)} %get-tuple-element.42.t), channel_id=1, source_target_pairs={{0,4},{1,5},{2,6},{3,7},{4,0},{5,1},{6,2},{7,3},{8,11},{9,13},{10,... | collective-permute-start | bytes 147464 | tf_op jit(solution)/shard_map/ppermute | solution.py:376
  42.3 1.2 %collective-permute-start.23 = (f32[16,768]{1,0:T(8,128)S(1)}, f32[16,768]{1,0:T(8,128)S(1)}, u32[]{:S(2)}, u32[]{:S(2)}) collective-permute-start(f32[16,768]{1,0:T(8,128)S(1)} %get-tuple-element.42.t), channel_id=1, source_target_pairs={{0,4},{1,5},{2,6},{3,7},{4,0},{5,1},{6,2},{7,3},{8,10},{9,13},{10,... | collective-permute-start | bytes 147464 | tf_op jit(solution)/shard_map/ppermute | solution.py:376
  42.3 1.4 %collective-permute-start.22 = (f32[16,768]{1,0:T(8,128)S(1)}, f32[16,768]{1,0:T(8,128)S(1)}, u32[]{:S(2)}, u32[]{:S(2)}) collective-permute-start(f32[16,768]{1,0:T(8,128)S(1)} %get-tuple-element.42.t), channel_id=1, source_target_pairs={{0,4},{1,5},{2,6},{3,7},{4,0},{5,1},{6,2},{7,3},{8,9},{9,13},{10,1... | collective-permute-start | bytes 147464 | tf_op jit(solution)/shard_map/ppermute | solution.py:376
  43.8 1.3 %collective-permute-start.25 = (f32[16,768]{1,0:T(8,128)S(1)}, f32[16,768]{1,0:T(8,128)S(1)}, u32[]{:S(2)}, u32[]{:S(2)}) collective-permute-start(f32[16,768]{1,0:T(8,128)S(1)} %shard_map.65.own), channel_id=1, source_target_pairs={{0,4},{4,0},{8,12},{12,8},{16,20},{20,16},{24,28},{28,24},{1,5},{5... | collective-permute-start | bytes 147464 | tf_op jit(solution)/shard_map/ppermute | solution.py:389
  46.8 1.7 %collective-permute-start.26 = (bf16[4,16,1024]{2,1,0:T(8,128)(2,1)S(1)}, bf16[4,16,1024]{2,1,0:T(8,128)(2,1)S(1)}, u32[]{:S(2)}, u32[]{:S(2)}) collective-permute-start(bf16[4,16,1024]{2,1,0:T(8,128)(2,1)S(1)} %shard_map.68), channel_id=1, source_target_pairs={{0,4},{4,0},{8,12},{12,8},{16,20},{20,16},{24,28},{28,24},{1,5},{5... | collective-permute-start | bytes 393224 | tf_op jit(solution)/shard_map/ppermute | solution.py:196
  48.5 5.4 %collective-permute-start.27 = (bf16[16,1024]{1,0:T(8,128)(2,1)S(1)}, bf16[16,1024]{1,0:T(8,128)(2,1)S(1)}, u32[]{:S(2)}, u32[]{:S(2)}) collective-permute-start(bf16[16,1024]{1,0:T(8,128)(2,1)S(1)} %get-tuple-element.46), channel_id=1, source_target_pairs={{0,8},{4,12},{8,0},{12,4},{16,24},{20,28},{24,16},{28,20},{1,9},{5... | collective-permute-start | bytes 98312 | tf_op jit(solution)/shard_map/ppermute | solution.py:196
  52.0 3.9 %collective-permute-start.28 = (bf16[16,1024]{1,0:T(8,128)(2,1)S(1)}, bf16[16,1024]{1,0:T(8,128)(2,1)S(1)}, u32[]{:S(2)}, u32[]{:S(2)}) collective-permute-start(bf16[16,1024]{1,0:T(8,128)(2,1)S(1)} %get-tuple-element.47), channel_id=1, source_target_pairs={{0,16},{4,20},{8,24},{12,28},{16,0},{20,4},{24,8},{28,12},{1,17},{... | collective-permute-start | bytes 98312 | tf_op jit(solution)/shard_map/ppermute | solution.py:196
  53.3 4.8 %collective-permute-start.29 = (bf16[16,1024]{1,0:T(8,128)(2,1)S(1)}, bf16[16,1024]{1,0:T(8,128)(2,1)S(1)}, u32[]{:S(2)}, u32[]{:S(2)}) collective-permute-start(bf16[16,1024]{1,0:T(8,128)(2,1)S(1)} %get-tuple-element.48), channel_id=1, source_target_pairs={{0,24},{4,28},{8,16},{12,20},{16,8},{20,12},{24,0},{28,4},{1,25},{... | collective-permute-start | bytes 98312 | tf_op jit(solution)/shard_map/ppermute | solution.py:196
  (1 other events, 9.3 us)

commit v3 on v2

--- a/solution.py
+++ b/solution.py
@@ -14,7 +14,6 @@
 F32 = jnp.float32
 BF16 = jnp.bfloat16
 VMEM = pl.BlockSpec(memory_space=pltpu.VMEM)
-SMEM = pl.BlockSpec(memory_space=pltpu.SMEM)
 HBM = pl.BlockSpec(memory_space=pltpu.HBM)
 MIB = 1024 * 1024
 NN = (((1,), (0,)), ((), ()))
@@ -57,7 +56,7 @@
 
 
 def fit(
-    screen_in, densities_in, integrals, left, right, out, screen, densities, total, arrived
+    screen_in, densities_in, integrals, left, right, out, masks, screen, densities, total, arrived
 ):
     height, width = integrals.shape
     pieces = arrived.shape[0] - 2
@@ -84,6 +83,10 @@
         copy.wait()
     count = densities.shape[0]
     strips = height // TILE
+    for i in range(strips):
+        for t in range(width // TILE):
+            flag = jnp.where(screen[i, t] != 0, 1.0, 0.0)
+            masks[i : i + 1, t * TILE : (t + 1) * TILE] = jnp.full((1, TILE), flag, F32)
     for j in range(pieces):
         tiles = range(j * chunk // TILE, (j + 1) * chunk // TILE)
         stacked = jnp.concatenate([masked_row(screen, densities, i, tiles) for i in range(strips)])
@@ -102,7 +105,8 @@
     pieces = 4 if width % (4 * TILE) == 0 else width // TILE
     return call(
         fit,
-        [struct((height, width // 2), BF16)] * 2 + [struct((count, height))],
+        [struct((height, width // 2), BF16)] * 2
+        + [struct((count, height)), struct((height // TILE, width))],
         *(pltpu.with_memory_space_constraint(x, pltpu.HBM) for x in (screen, densities, integrals)),
         specs=[HBM] * 3,
         scratch=[
@@ -114,21 +118,18 @@
     )
 
 
-def slab(screen, stacked, left, right, member, members):
+def slab(masks, stacked, left, right, member, members):
     strips = left.shape[0] // TILE
     count = stacked.shape[0] // strips
     chunk = 2 * left.shape[1] // members
     held, first = (left, member) if 2 * member < members else (right, member - members // 2)
     columns = slice(first * chunk, (first + 1) * chunk)
     parts = jnp.dot(stacked, held[:, columns], preferred_element_type=F32)
-    tiles = []
-    for t in range(chunk // TILE):
-        total = jnp.zeros((count, TILE), F32)
-        for i in range(strips):
-            part = parts[i * count : (i + 1) * count, t * TILE : (t + 1) * TILE]
-            total += jnp.where(screen[i, member * (chunk // TILE) + t] != 0, part, 0.0)
-        tiles.append(total)
-    return jnp.concatenate(tiles, axis=1)
+    total = jnp.zeros((count, chunk), F32)
+    for i in range(strips):
+        mask = masks[i : i + 1, member * chunk : (member + 1) * chunk]
+        total += jnp.where(mask != 0, parts[i * count : (i + 1) * count], 0.0)
+    return total
 
 
 def by_strip(value, strips):
@@ -138,20 +139,20 @@
     )
 
 
-def coulomb(screen, rounded, left, right, out):
+def coulomb(masks, rounded, left, right, out):
     members = out.shape[0]
     stacked = by_strip(rounded[...], left.shape[0] // TILE)
     for m in range(members):
-        out[m] = slab(screen, stacked, left, right, m, members).astype(out.dtype)
-
-
-def coulomb_side(wanted, screen, rounded, left, right, out):
+        out[m] = slab(masks, stacked, left, right, m, members).astype(out.dtype)
+
+
+def coulomb_side(wanted, masks, rounded, left, right, out):
     chips = out.shape[0]
     stacked = by_strip(rounded[...], left.shape[0] // TILE)
 
     def compute(side):
         for k in range(chips):
-            part = slab(screen, stacked, left, right, 2 * k + side, 2 * chips)
+            part = slab(masks, stacked, left, right, 2 * k + side, 2 * chips)
             out[k] = part.astype(out.dtype)
 
     for side in range(2):
@@ -178,25 +179,24 @@
     out[...] = keep[...] + one[...].astype(F32) + two[...].astype(F32) + three[...].astype(F32)
 
 
-def coulomb_partial(rounded, left, right, screen):
+def coulomb_partial(rounded, left, right, masks):
     members = lax.axis_size("aux")
     out = struct((members, rounded.shape[0], 2 * left.shape[1] // members), BF16)
-    return call(coulomb, out, screen, rounded, left, right, specs=[SMEM, VMEM, VMEM, VMEM])
-
-
-def chip_coulomb(rounded, left, right, screen):
+    return call(coulomb, out, masks, rounded, left, right)
+
+
+def chip_coulomb(rounded, left, right, masks):
     members = 2 * SOLVE_BLOCKS
     count = rounded.shape[0]
     chunk = 2 * left.shape[1] // members
-    specs = [SMEM, VMEM, VMEM, VMEM]
-    operands = (screen, rounded, left, right)
-    given = call(coulomb_mate, struct((SOLVE_BLOCKS, count, chunk), BF16), *operands, specs=specs)
+    operands = (masks, rounded, left, right)
+    given = call(coulomb_mate, struct((SOLVE_BLOCKS, count, chunk), BF16), *operands)
 
     def move(value, to):
         return lax.ppermute(value, "aux", [(i, to(i)) for i in range(members)])
 
     got = move(given, lambda i: i ^ 1)
-    own = call(coulomb_own, struct((SOLVE_BLOCKS, count, chunk)), *operands, specs=specs)
+    own = call(coulomb_own, struct((SOLVE_BLOCKS, count, chunk)), *operands)
     piece = struct((count, chunk), BF16)
     keep, one, two, three = call(share, [struct((count, chunk))] + [piece] * 3, own, got)
     three = move(three, lambda i: i ^ 6)
@@ -526,11 +526,11 @@
         and lax.axis_size("pair") == SOLVE_BLOCKS
     )
     solve = chip_solve if chip_blocks else chain_solve
-    left, right, partial_fit = fit_partial(densities, integrals, screen)
+    left, right, partial_fit, masks = fit_partial(densities, integrals, screen)
     rounded = solve(partial_fit, factor, diag_inv)
     if chip_blocks:
-        return chip_coulomb(rounded, left, right, screen)
-    return scatter_sum(coulomb_partial(rounded, left, right, screen))
+        return chip_coulomb(rounded, left, right, masks)
+    return scatter_sum(coulomb_partial(rounded, left, right, masks))
 
 
 def solution(mesh):

time: 58.9 us -> 58.1 us (0.986)
  Pallas kernels: 11 us -> 9.83 us
    pallas_call x16, Pallas kernels: 11 us -> 9.83 us  [call(): pl.pallas_call(kernel, out_shape=outs, in_specs=specs or [VMEM] * len(ope...]
  transfers between devices with their start and end apart: 30 -> 30, of which waited for: 22 -> 23; matrix products, arithmetic and copies ran while one was open for 0% -> 0% of each run, Pallas kernels for 9% -> 8%
where the time goes in v3:
time: 58.1 us; the launch traced here: 58 us
  starting transfers between devices  26.1 us (45%)
  waiting for transfers between devices  21.9 us (38%)
  Pallas kernels  9.83 us (17%)
    ppermute x22, starting transfers between devices, permute(): return lax.ppermute(value, AXES, sorted(to.items()))  19.6 us
    ppermute x22, waiting for transfers between devices, permute(): return lax.ppermute(value, AXES, sorted(to.items()))  14.9 us
    pallas_call x16, Pallas kernels, call(): pl.pallas_call(kernel, out_shape=outs, in_specs=specs or [VMEM] * len(ope...  9.83 us
    ppermute x4, starting transfers between devices, move(): return lax.ppermute(value, 'aux', [(i, to(i)) for i in range(members)])  5.5 us
    ppermute x4, waiting for transfers between devices, move(): return lax.ppermute(value, 'aux', [(i, to(i)) for i in range(members)])  4.89 us
    ppermute x4, waiting for transfers between devices, swap(): lax.ppermute(value, 'aux', [(i, i ^ 1) for i in range(2 * SOLVE_BLOCKS)])  2.14 us
  transfers between devices with their start and end apart: 30, of which 23 were waited for; matrix products, arithmetic and copies ran while one was open for 0% of the time, Pallas kernels for 8%

profile of v3, /device:TPU:0, one launch (start us, length us, event | category | flops | bytes accessed | tf_op | source)
XLA Modules:
  0.0 58.0 jit_solution(4123242715302734884)
XLA Ops:
  0.0 0.5 collective-permute-start.4
  0.6 4.0 %shard_map.55 = (bf16[384,4096]{1,0:T(8,128)(2,1)S(1)}, bf16[384,4096]{1,0:T(8,128)(2,1)S(1)}, f32[16,384]{1,0:T(8,128)S(1)}, f32[3,8192]{1,0:T(4,128)S(1)}) custom-call(s32[3,64]{1,0:T(4,128)} %screen_in.1, bf16[16,8192]{1,0:T(8,128)(2,1)} %densities_in.1, bf16[384,8192]{1,0:T(8,128)(2,1)} %integrals.1), custom_call_target="tpu_custom_call" | custom-call | tf_op jit(solution)/shard_map/pallas_call | solution.py:29
  4.6 0.6 collective-permute-start.2
  5.1 4.1 %collective-permute-start.1 = (f32[16,384]{1,0:T(8,128)S(1)}, f32[16,384]{1,0:T(8,128)S(1)}, u32[]{:S(2)}, u32[]{:S(2)}) collective-permute-start(f32[16,384]{1,0:T(8,128)S(1)} %get-tuple-element.29.f0), channel_id=1, source_target_pairs={{0,1},{1,0},{2,6},{3,7},{4,5},{5,4},{6,2},{7,3},{8,9},{9,8},{10,14... | collective-permute-start | bytes 73736 | tf_op jit(solution)/shard_map/ppermute | solution.py:376
  9.3 1.7 %collective-permute-done.1.f2 = f32[16,384]{1,0:T(8,128)S(1)} collective-permute-done((f32[16,384]{1,0:T(8,128)S(1)}, f32[16,384]{1,0:T(8,128)S(1)}, u32[]{:S(2)}, u32[]{:S(2)}) %collective-permute-start.1) | collective-permute-done | bytes 24608 | tf_op jit(solution)/shard_map/ppermute | solution.py:376
  11.4 1.2 %collective-permute-done.5.mate = f32[16,768]{1,0:T(8,128)S(1)} collective-permute-done((f32[16,768]{1,0:T(8,128)S(1)}, f32[16,768]{1,0:T(8,128)S(1)}, u32[]{:S(2)}, u32[]{:S(2)}) %collective-permute-start.5) | collective-permute-done | bytes 49184 | tf_op jit(solution)/shard_map/ppermute | solution.py:389
  13.3 0.6 %collective-permute-done.8.three = f32[16,768]{1,0:T(8,128)S(1)} collective-permute-done((f32[16,768]{1,0:T(8,128)S(1)}, f32[16,768]{1,0:T(8,128)S(1)}, u32[]{:S(2)}, u32[]{:S(2)}) %collective-permute-start.8) | collective-permute-done | bytes 49184 | tf_op jit(solution)/shard_map/ppermute | solution.py:376
  15.0 0.5 collective-permute-start.9
  15.5 0.7 %collective-permute-done.10.second.z2 = f32[16,768]{1,0:T(8,128)S(1)} collective-permute-done((f32[16,768]{1,0:T(8,128)S(1)}, f32[16,768]{1,0:T(8,128)S(1)}, u32[]{:S(2)}, u32[]{:S(2)}) %collective-permute-start.10) | collective-permute-done | bytes 49184 | tf_op jit(solution)/shard_map/ppermute | solution.py:376
  16.2 6.6 %collective-permute-done.9.first.z0 = f32[16,768]{1,0:T(8,128)S(1)} collective-permute-done((f32[16,768]{1,0:T(8,128)S(1)}, f32[16,768]{1,0:T(8,128)S(1)}, u32[]{:S(2)}, u32[]{:S(2)}) %collective-permute-start.9) | collective-permute-done | bytes 49184 | tf_op jit(solution)/shard_map/ppermute | solution.py:376
  23.3 0.5 collective-permute-start.11
  23.8 0.7 %collective-permute-done.12.known = f32[16,768]{1,0:T(8,128)S(1)} collective-permute-done((f32[16,768]{1,0:T(8,128)S(1)}, f32[16,768]{1,0:T(8,128)S(1)}, u32[]{:S(2)}, u32[]{:S(2)}) %collective-permute-start.12) | collective-permute-done | bytes 49184 | tf_op jit(solution)/shard_map/ppermute | solution.py:376
  24.6 1.0 %shard_map.62 = (f32[16,768]{1,0:T(8,128)S(1)}, f32[16,768]{1,0:T(8,128)S(1)}) custom-call(f32[16,768]{1,0:T(8,128)S(1)} %collective-permute-done.12.known, f32[16,768]{1,0:T(8,128)S(1)} %collective-permute-done.11.behind.z3, f32[16,768]{1,0:T(8,128)S(1)} %shard_map.58.e.z1, bf16[768,768]{1,0:T(8,128)(2,1)S(1)} %get-tuple-element.33.high.kt_high, ...), custom_call_target="tpu_custom_call" | custom-call | tf_op jit(solution)/shard_map/pallas_call | solution.py:29
  25.7 0.5 collective-permute-start.15
  26.2 0.7 %collective-permute-done.13.into = f32[16,768]{1,0:T(8,128)S(1)} collective-permute-done((f32[16,768]{1,0:T(8,128)S(1)}, f32[16,768]{1,0:T(8,128)S(1)}, u32[]{:S(2)}, u32[]{:S(2)}) %collective-permute-start.13) | collective-permute-done | bytes 49184 | tf_op jit(solution)/shard_map/ppermute | solution.py:376
  27.4 0.5 shard_map.63
  27.9 0.5 collective-permute-start.17
  28.4 0.7 %collective-permute-done.16.into = f32[16,768]{1,0:T(8,128)S(1)} collective-permute-done((f32[16,768]{1,0:T(8,128)S(1)}, f32[16,768]{1,0:T(8,128)S(1)}, u32[]{:S(2)}, u32[]{:S(2)}) %collective-permute-start.16) | collective-permute-done | bytes 49184 | tf_op jit(solution)/shard_map/ppermute | solution.py:376
  29.8 3.8 %collective-permute-start.20 = (f32[16,768]{1,0:T(8,128)S(1)}, f32[16,768]{1,0:T(8,128)S(1)}, u32[]{:S(2)}, u32[]{:S(2)}) collective-permute-start(f32[16,768]{1,0:T(8,128)S(1)} %get-tuple-element.43), channel_id=1, source_target_pairs={{0,4},{1,5},{2,6},{3,7},{4,0},{5,1},{6,9},{7,17},{8,2},{9,13},{10,... | collective-permute-start | bytes 147464 | tf_op jit(solution)/shard_map/ppermute | solution.py:376
  33.6 0.5 collective-permute-start.18
  34.2 7.3 %collective-permute-start.24 = (f32[16,768]{1,0:T(8,128)S(1)}, f32[16,768]{1,0:T(8,128)S(1)}, u32[]{:S(2)}, u32[]{:S(2)}) collective-permute-start(f32[16,768]{1,0:T(8,128)S(1)} %get-tuple-element.44.t), channel_id=1, source_target_pairs={{0,4},{1,5},{2,6},{3,7},{4,0},{5,1},{6,2},{7,3},{8,11},{9,13},{10,... | collective-permute-start | bytes 147464 | tf_op jit(solution)/shard_map/ppermute | solution.py:376
  41.5 0.8 %collective-permute-done.21.i3 = f32[16,768]{1,0:T(8,128)S(1)} collective-permute-done((f32[16,768]{1,0:T(8,128)S(1)}, f32[16,768]{1,0:T(8,128)S(1)}, u32[]{:S(2)}, u32[]{:S(2)}) %collective-permute-start.21) | collective-permute-done | bytes 49184 | tf_op jit(solution)/shard_map/ppermute | solution.py:376
  42.3 0.5 collective-permute-start.22
  42.8 0.6 collective-permute-done.18.i0
  44.2 0.9 %collective-permute-done.25.mate = f32[16,768]{1,0:T(8,128)S(1)} collective-permute-done((f32[16,768]{1,0:T(8,128)S(1)}, f32[16,768]{1,0:T(8,128)S(1)}, u32[]{:S(2)}, u32[]{:S(2)}) %collective-permute-start.25) | collective-permute-done | bytes 49184 | tf_op jit(solution)/shard_map/ppermute | solution.py:389
  45.5 0.7 %shard_map.68 = bf16[4,16,1024]{2,1,0:T(8,128)(2,1)S(1)} custom-call(f32[3,8192]{1,0:T(4,128)S(1)} %get-tuple-element.28.refs_0_, bf16[16,384]{1,0:T(8,128)(2,1)S(1)} %shard_map.66.refs_1_, bf16[384,4096]{1,0:T(8,128)(2,1)S(1)} %get-tuple-element.45.refs_2_, bf16[384,4096]{1,0:T(8,128)(2,1)S(1)} %get-tuple-element.46.refs_3_), custom_call_target="tpu_custom_call" | custom-call | tf_op jit(solution)/shard_map/pallas_call | solution.py:29
  46.6 0.7 %shard_map.67.own = f32[4,16,1024]{2,1,0:T(8,128)S(1)} custom-call(f32[3,8192]{1,0:T(4,128)S(1)} %get-tuple-element.28.refs_0_, bf16[16,384]{1,0:T(8,128)(2,1)S(1)} %shard_map.66.refs_1_, bf16[384,4096]{1,0:T(8,128)(2,1)S(1)} %get-tuple-element.45.refs_2_, bf16[384,4096]{1,0:T(8,128)(2,1)S(1)} %get-tuple-element.46.refs_3_), custom_call_target="tpu_custom_call" | custom-call | tf_op jit(solution)/shard_map/pallas_call | solution.py:29
  47.7 3.5 %collective-permute-start.27 = (bf16[16,1024]{1,0:T(8,128)(2,1)S(1)}, bf16[16,1024]{1,0:T(8,128)(2,1)S(1)}, u32[]{:S(2)}, u32[]{:S(2)}) collective-permute-start(bf16[16,1024]{1,0:T(8,128)(2,1)S(1)} %get-tuple-element.48), channel_id=1, source_target_pairs={{0,8},{4,12},{8,0},{12,4},{16,24},{20,28},{24,16},{28,20},{1,9},{5... | collective-permute-start | bytes 98312 | tf_op jit(solution)/shard_map/ppermute | solution.py:196
  51.2 1.3 %collective-permute-start.28 = (bf16[16,1024]{1,0:T(8,128)(2,1)S(1)}, bf16[16,1024]{1,0:T(8,128)(2,1)S(1)}, u32[]{:S(2)}, u32[]{:S(2)}) collective-permute-start(bf16[16,1024]{1,0:T(8,128)(2,1)S(1)} %get-tuple-element.49), channel_id=1, source_target_pairs={{0,16},{4,20},{8,24},{12,28},{16,0},{20,4},{24,8},{28,12},{1,17},{... | collective-permute-start | bytes 98312 | tf_op jit(solution)/shard_map/ppermute | solution.py:196
  53.1 2.0 %collective-permute-done.28.two = bf16[16,1024]{1,0:T(8,128)(2,1)S(1)} collective-permute-done((bf16[16,1024]{1,0:T(8,128)(2,1)S(1)}, bf16[16,1024]{1,0:T(8,128)(2,1)S(1)}, u32[]{:S(2)}, u32[]{:S(2)}) %collective-permute-start.28) | collective-permute-done | bytes 32800 | tf_op jit(solution)/shard_map/ppermute | solution.py:196
  55.1 2.2 %collective-permute-done.29.three = bf16[16,1024]{1,0:T(8,128)(2,1)S(1)} collective-permute-done((bf16[16,1024]{1,0:T(8,128)(2,1)S(1)}, bf16[16,1024]{1,0:T(8,128)(2,1)S(1)}, u32[]{:S(2)}, u32[]{:S(2)}) %collective-permute-start.29) | collective-permute-done | bytes 32800 | tf_op jit(solution)/shard_map/ppermute | solution.py:196
  57.3 0.6 %shard_map.70 = f32[16,1024]{1,0:T(8,128)} custom-call(f32[16,1024]{1,0:T(8,128)S(1)} %get-tuple-element.47.keep, bf16[16,1024]{1,0:T(8,128)(2,1)S(1)} %collective-permute-done.27.one, bf16[16,1024]{1,0:T(8,128)(2,1)S(1)} %collective-permute-done.28.two, bf16[16,1024]{1,0:T(8,128)(2,1)S(1)} %collective-permute-done.29.three), custom_call_target="tpu_custom_call" | custom-call | tf_op jit(solution)/shard_map/pallas_call | solution.py:29
  (48 shorter events, 6.5 us)
Async XLA Ops:
  0.0 9.3 %copy-start.1 = (f32[384,768]{1,0:T(8,128)S(1)}, f32[384,768]{1,0:T(8,128)}, u32[]{:S(2)}) copy-start(f32[384,768]{1,0:T(8,128)} %refs_2_.3) | copy-start | bytes 3538948
  0.0 9.3 %copy-start = (f32[384,768]{1,0:T(8,128)S(1)}, f32[384,768]{1,0:T(8,128)}, u32[]{:S(2)}) copy-start(f32[384,768]{1,0:T(8,128)} %inv.3) | copy-start | bytes 3538948
  0.0 9.3 %collective-permute-start.4 = (f32[384,768]{1,0:T(8,128)}, f32[384,768]{1,0:T(8,128)S(1)}, u32[]{:S(2)}, u32[]{:S(2)}) collective-permute-start(f32[384,768]{1,0:T(8,128)} %refs_2_.3), channel_id=1, source_target_pairs={{0,4},{4,0},{8,12},{12,8},{16,20},{20,16},{24,28},{28,24},{1,5},{5... | collective-permute-start | bytes 3538952 | tf_op jit(solution)/shard_map/ppermute | solution.py:389
  0.5 8.8 %collective-permute-start.3 = (f32[384,768]{1,0:T(8,128)}, f32[384,768]{1,0:T(8,128)S(1)}, u32[]{:S(2)}, u32[]{:S(2)}) collective-permute-start(f32[384,768]{1,0:T(8,128)} %inv.3), channel_id=1, source_target_pairs={{0,4},{4,0},{8,12},{12,8},{16,20},{20,16},{24,28},{28,24},{1,5},{5... | collective-permute-start | bytes 3538952 | tf_op jit(solution)/shard_map/ppermute | solution.py:389
  4.6 4.8 %collective-permute-start.2 = (f32[16,384]{1,0:T(8,128)S(1)}, f32[16,384]{1,0:T(8,128)S(1)}, u32[]{:S(2)}, u32[]{:S(2)}) collective-permute-start(f32[16,384]{1,0:T(8,128)S(1)} %get-tuple-element.29.f0), channel_id=1, source_target_pairs={{0,4},{1,2},{2,1},{3,7},{4,0},{5,6},{6,5},{7,3},{8,12},{9,10},{10,... | collective-permute-start | bytes 73736 | tf_op jit(solution)/shard_map/ppermute | solution.py:376
  5.1 5.9 %collective-permute-start.1 = (f32[16,384]{1,0:T(8,128)S(1)}, f32[16,384]{1,0:T(8,128)S(1)}, u32[]{:S(2)}, u32[]{:S(2)}) collective-permute-start(f32[16,384]{1,0:T(8,128)S(1)} %get-tuple-element.29.f0), channel_id=1, source_target_pairs={{0,1},{1,0},{2,6},{3,7},{4,5},{5,4},{6,2},{7,3},{8,9},{9,8},{10,14... | collective-permute-start | bytes 73736 | tf_op jit(solution)/shard_map/ppermute | solution.py:376
  9.3 1.8 %collective-permute-start = (f32[16,384]{1,0:T(8,128)S(1)}, f32[16,384]{1,0:T(8,128)S(1)}, u32[]{:S(2)}, u32[]{:S(2)}) collective-permute-start(f32[16,384]{1,0:T(8,128)S(1)} %get-tuple-element.29.f0), channel_id=1, source_target_pairs={{0,4},{1,2},{2,3},{3,1},{4,0},{5,6},{6,7},{7,5},{8,12},{9,10},{10,... | collective-permute-start | bytes 73736 | tf_op jit(solution)/shard_map/ppermute | solution.py:376
  11.4 1.3 %collective-permute-start.5 = (f32[16,768]{1,0:T(8,128)S(1)}, f32[16,768]{1,0:T(8,128)S(1)}, u32[]{:S(2)}, u32[]{:S(2)}) collective-permute-start(f32[16,768]{1,0:T(8,128)S(1)} %shard_map.57.own), channel_id=1, source_target_pairs={{0,4},{4,0},{8,12},{12,8},{16,20},{20,16},{24,28},{28,24},{1,5},{5... | collective-permute-start | bytes 147464 | tf_op jit(solution)/shard_map/ppermute | solution.py:389
  12.6 1.3 %collective-permute-start.8 = (f32[16,768]{1,0:T(8,128)S(1)}, f32[16,768]{1,0:T(8,128)S(1)}, u32[]{:S(2)}, u32[]{:S(2)}) collective-permute-start(f32[16,768]{1,0:T(8,128)S(1)} %shard_map.58.e.z1), channel_id=1, source_target_pairs={{0,4},{1,24},{2,6},{3,7},{4,0},{5,1},{6,2},{7,3},{8,12},{9,13},{10... | collective-permute-start | bytes 147464 | tf_op jit(solution)/shard_map/ppermute | solution.py:376
  12.8 1.3 %collective-permute-start.7 = (f32[16,768]{1,0:T(8,128)S(1)}, f32[16,768]{1,0:T(8,128)S(1)}, u32[]{:S(2)}, u32[]{:S(2)}) collective-permute-start(f32[16,768]{1,0:T(8,128)S(1)} %shard_map.58.e.z1), channel_id=1, source_target_pairs={{0,4},{1,16},{2,6},{3,7},{4,0},{5,1},{6,2},{7,3},{8,12},{9,8},{10,... | collective-permute-start | bytes 147464 | tf_op jit(solution)/shard_map/ppermute | solution.py:376
  13.2 1.2 %collective-permute-start.6 = (f32[16,768]{1,0:T(8,128)S(1)}, f32[16,768]{1,0:T(8,128)S(1)}, u32[]{:S(2)}, u32[]{:S(2)}) collective-permute-start(f32[16,768]{1,0:T(8,128)S(1)} %shard_map.58.e.z1), channel_id=1, source_target_pairs={{0,4},{1,8},{2,6},{3,7},{4,0},{5,1},{6,2},{7,3},{8,12},{9,13},{10,... | collective-permute-start | bytes 147464 | tf_op jit(solution)/shard_map/ppermute | solution.py:376
  14.9 1.2 %collective-permute-start.10 = (f32[16,768]{1,0:T(8,128)S(1)}, f32[16,768]{1,0:T(8,128)S(1)}, u32[]{:S(2)}, u32[]{:S(2)}) collective-permute-start(f32[16,768]{1,0:T(8,128)S(1)} %shard_map.60.s), channel_id=1, source_target_pairs={{0,4},{1,2},{2,6},{3,7},{4,0},{5,1},{6,5},{7,3},{8,25},{9,13},{10,... | collective-permute-start | bytes 147464 | tf_op jit(solution)/shard_map/ppermute | solution.py:376
  15.0 7.8 %collective-permute-start.9 = (f32[16,768]{1,0:T(8,128)S(1)}, f32[16,768]{1,0:T(8,128)S(1)}, u32[]{:S(2)}, u32[]{:S(2)}) collective-permute-start(f32[16,768]{1,0:T(8,128)S(1)} %shard_map.60.s), channel_id=1, source_target_pairs={{0,4},{1,0},{2,6},{3,7},{4,5},{5,1},{6,2},{7,3},{8,17},{9,13},{10,... | collective-permute-start | bytes 147464 | tf_op jit(solution)/shard_map/ppermute | solution.py:376
  23.2 1.2 %collective-permute-start.12 = (f32[16,768]{1,0:T(8,128)S(1)}, f32[16,768]{1,0:T(8,128)S(1)}, u32[]{:S(2)}, u32[]{:S(2)}) collective-permute-start(f32[16,768]{1,0:T(8,128)S(1)} %shard_map.61.s), channel_id=1, source_target_pairs={{0,4},{1,5},{2,6},{3,7},{4,0},{5,1},{6,2},{7,3},{8,12},{9,13},{10,... | collective-permute-start | bytes 147464 | tf_op jit(solution)/shard_map/ppermute | solution.py:376
  23.3 1.4 %collective-permute-start.11 = (f32[16,768]{1,0:T(8,128)S(1)}, f32[16,768]{1,0:T(8,128)S(1)}, u32[]{:S(2)}, u32[]{:S(2)}) collective-permute-start(f32[16,768]{1,0:T(8,128)S(1)} %shard_map.61.s), channel_id=1, source_target_pairs={{0,4},{1,3},{2,6},{3,7},{4,0},{5,1},{6,2},{7,5},{8,12},{9,13},{10,... | collective-permute-start | bytes 147464 | tf_op jit(solution)/shard_map/ppermute | solution.py:376
  25.7 1.2 %collective-permute-start.13 = (f32[16,768]{1,0:T(8,128)S(1)}, f32[16,768]{1,0:T(8,128)S(1)}, u32[]{:S(2)}, u32[]{:S(2)}) collective-permute-start(f32[16,768]{1,0:T(8,128)S(1)} %get-tuple-element.36), channel_id=1, source_target_pairs={{0,4},{1,5},{2,6},{3,7},{4,0},{5,1},{6,2},{7,3},{8,12},{9,13},{10,... | collective-permute-start | bytes 147464 | tf_op jit(solution)/shard_map/ppermute | solution.py:376
  25.7 1.4 %collective-permute-start.15 = (f32[16,768]{1,0:T(8,128)S(1)}, f32[16,768]{1,0:T(8,128)S(1)}, u32[]{:S(2)}, u32[]{:S(2)}) collective-permute-start(f32[16,768]{1,0:T(8,128)S(1)} %get-tuple-element.37.t), channel_id=1, source_target_pairs={{0,4},{1,5},{2,6},{3,7},{4,0},{5,1},{6,2},{7,3},{8,12},{9,13},{10,... | collective-permute-start | bytes 147464 | tf_op jit(solution)/shard_map/ppermute | solution.py:376
  26.2 1.2 %collective-permute-start.14 = (f32[16,768]{1,0:T(8,128)S(1)}, f32[16,768]{1,0:T(8,128)S(1)}, u32[]{:S(2)}, u32[]{:S(2)}) collective-permute-start(f32[16,768]{1,0:T(8,128)S(1)} %get-tuple-element.37.t), channel_id=1, source_target_pairs={{0,4},{1,5},{2,6},{3,7},{4,0},{5,1},{6,2},{7,3},{8,12},{9,13},{10,... | collective-permute-start | bytes 147464 | tf_op jit(solution)/shard_map/ppermute | solution.py:376
  27.9 1.2 %collective-permute-start.16 = (f32[16,768]{1,0:T(8,128)S(1)}, f32[16,768]{1,0:T(8,128)S(1)}, u32[]{:S(2)}, u32[]{:S(2)}) collective-permute-start(f32[16,768]{1,0:T(8,128)S(1)} %get-tuple-element.40), channel_id=1, source_target_pairs={{0,4},{1,5},{2,6},{3,7},{4,0},{5,1},{6,2},{7,3},{8,12},{9,13},{10,... | collective-permute-start | bytes 147464 | tf_op jit(solution)/shard_map/ppermute | solution.py:376
  27.9 1.4 %collective-permute-start.17 = (f32[16,768]{1,0:T(8,128)S(1)}, f32[16,768]{1,0:T(8,128)S(1)}, u32[]{:S(2)}, u32[]{:S(2)}) collective-permute-start(f32[16,768]{1,0:T(8,128)S(1)} %get-tuple-element.41), channel_id=1, source_target_pairs={{0,4},{1,5},{2,6},{3,7},{4,0},{5,1},{6,2},{7,3},{8,12},{9,13},{10,... | collective-permute-start | bytes 147464 | tf_op jit(solution)/shard_map/ppermute | solution.py:376
  29.8 12.5 %collective-permute-start.21 = (f32[16,768]{1,0:T(8,128)S(1)}, f32[16,768]{1,0:T(8,128)S(1)}, u32[]{:S(2)}, u32[]{:S(2)}) collective-permute-start(f32[16,768]{1,0:T(8,128)S(1)} %get-tuple-element.43), channel_id=1, source_target_pairs={{0,4},{1,5},{2,6},{3,7},{4,18},{5,1},{6,2},{7,24},{8,3},{9,13},{10... | collective-permute-start | bytes 147464 | tf_op jit(solution)/shard_map/ppermute | solution.py:376
  29.8 12.5 %collective-permute-start.20 = (f32[16,768]{1,0:T(8,128)S(1)}, f32[16,768]{1,0:T(8,128)S(1)}, u32[]{:S(2)}, u32[]{:S(2)}) collective-permute-start(f32[16,768]{1,0:T(8,128)S(1)} %get-tuple-element.43), channel_id=1, source_target_pairs={{0,4},{1,5},{2,6},{3,7},{4,0},{5,1},{6,9},{7,17},{8,2},{9,13},{10,... | collective-permute-start | bytes 147464 | tf_op jit(solution)/shard_map/ppermute | solution.py:376
  33.6 9.2 %collective-permute-start.19 = (f32[16,768]{1,0:T(8,128)S(1)}, f32[16,768]{1,0:T(8,128)S(1)}, u32[]{:S(2)}, u32[]{:S(2)}) collective-permute-start(f32[16,768]{1,0:T(8,128)S(1)} %get-tuple-element.43), channel_id=1, source_target_pairs={{0,4},{1,5},{2,6},{3,7},{4,0},{5,12},{6,25},{7,3},{8,1},{9,13},{10... | collective-permute-start | bytes 147464 | tf_op jit(solution)/shard_map/ppermute | solution.py:376
  33.6 9.8 %collective-permute-start.18 = (f32[16,768]{1,0:T(8,128)S(1)}, f32[16,768]{1,0:T(8,128)S(1)}, u32[]{:S(2)}, u32[]{:S(2)}) collective-permute-start(f32[16,768]{1,0:T(8,128)S(1)} %get-tuple-element.43), channel_id=1, source_target_pairs={{0,4},{1,5},{2,6},{3,7},{4,12},{5,20},{6,2},{7,3},{8,0},{9,13},{10... | collective-permute-start | bytes 147464 | tf_op jit(solution)/shard_map/ppermute | solution.py:376
  34.2 9.2 %collective-permute-start.24 = (f32[16,768]{1,0:T(8,128)S(1)}, f32[16,768]{1,0:T(8,128)S(1)}, u32[]{:S(2)}, u32[]{:S(2)}) collective-permute-start(f32[16,768]{1,0:T(8,128)S(1)} %get-tuple-element.44.t), channel_id=1, source_target_pairs={{0,4},{1,5},{2,6},{3,7},{4,0},{5,1},{6,2},{7,3},{8,11},{9,13},{10,... | collective-permute-start | bytes 147464 | tf_op jit(solution)/shard_map/ppermute | solution.py:376
  42.3 1.2 %collective-permute-start.23 = (f32[16,768]{1,0:T(8,128)S(1)}, f32[16,768]{1,0:T(8,128)S(1)}, u32[]{:S(2)}, u32[]{:S(2)}) collective-permute-start(f32[16,768]{1,0:T(8,128)S(1)} %get-tuple-element.44.t), channel_id=1, source_target_pairs={{0,4},{1,5},{2,6},{3,7},{4,0},{5,1},{6,2},{7,3},{8,10},{9,13},{10,... | collective-permute-start | bytes 147464 | tf_op jit(solution)/shard_map/ppermute | solution.py:376
  42.3 1.4 %collective-permute-start.22 = (f32[16,768]{1,0:T(8,128)S(1)}, f32[16,768]{1,0:T(8,128)S(1)}, u32[]{:S(2)}, u32[]{:S(2)}) collective-permute-start(f32[16,768]{1,0:T(8,128)S(1)} %get-tuple-element.44.t), channel_id=1, source_target_pairs={{0,4},{1,5},{2,6},{3,7},{4,0},{5,1},{6,2},{7,3},{8,9},{9,13},{10,1... | collective-permute-start | bytes 147464 | tf_op jit(solution)/shard_map/ppermute | solution.py:376
  43.8 1.3 %collective-permute-start.25 = (f32[16,768]{1,0:T(8,128)S(1)}, f32[16,768]{1,0:T(8,128)S(1)}, u32[]{:S(2)}, u32[]{:S(2)}) collective-permute-start(f32[16,768]{1,0:T(8,128)S(1)} %shard_map.65.own), channel_id=1, source_target_pairs={{0,4},{4,0},{8,12},{12,8},{16,20},{20,16},{24,28},{28,24},{1,5},{5... | collective-permute-start | bytes 147464 | tf_op jit(solution)/shard_map/ppermute | solution.py:389
  46.2 1.4 %collective-permute-start.26 = (bf16[4,16,1024]{2,1,0:T(8,128)(2,1)S(1)}, bf16[4,16,1024]{2,1,0:T(8,128)(2,1)S(1)}, u32[]{:S(2)}, u32[]{:S(2)}) collective-permute-start(bf16[4,16,1024]{2,1,0:T(8,128)(2,1)S(1)} %shard_map.68), channel_id=1, source_target_pairs={{0,4},{4,0},{8,12},{12,8},{16,20},{20,16},{24,28},{28,24},{1,5},{5... | collective-permute-start | bytes 393224 | tf_op jit(solution)/shard_map/ppermute | solution.py:196
  47.7 5.4 %collective-permute-start.27 = (bf16[16,1024]{1,0:T(8,128)(2,1)S(1)}, bf16[16,1024]{1,0:T(8,128)(2,1)S(1)}, u32[]{:S(2)}, u32[]{:S(2)}) collective-permute-start(bf16[16,1024]{1,0:T(8,128)(2,1)S(1)} %get-tuple-element.48), channel_id=1, source_target_pairs={{0,8},{4,12},{8,0},{12,4},{16,24},{20,28},{24,16},{28,20},{1,9},{5... | collective-permute-start | bytes 98312 | tf_op jit(solution)/shard_map/ppermute | solution.py:196
  51.2 3.9 %collective-permute-start.28 = (bf16[16,1024]{1,0:T(8,128)(2,1)S(1)}, bf16[16,1024]{1,0:T(8,128)(2,1)S(1)}, u32[]{:S(2)}, u32[]{:S(2)}) collective-permute-start(bf16[16,1024]{1,0:T(8,128)(2,1)S(1)} %get-tuple-element.49), channel_id=1, source_target_pairs={{0,16},{4,20},{8,24},{12,28},{16,0},{20,4},{24,8},{28,12},{1,17},{... | collective-permute-start | bytes 98312 | tf_op jit(solution)/shard_map/ppermute | solution.py:196
  52.5 4.8 %collective-permute-start.29 = (bf16[16,1024]{1,0:T(8,128)(2,1)S(1)}, bf16[16,1024]{1,0:T(8,128)(2,1)S(1)}, u32[]{:S(2)}, u32[]{:S(2)}) collective-permute-start(bf16[16,1024]{1,0:T(8,128)(2,1)S(1)} %get-tuple-element.50), channel_id=1, source_target_pairs={{0,24},{4,28},{8,16},{12,20},{16,8},{20,12},{24,0},{28,4},{1,25},{... | collective-permute-start | bytes 98312 | tf_op jit(solution)/shard_map/ppermute | solution.py:196
